TPU v7x, 32 devices: a whole 2x2x4 slice. The times are simulated.
32 devices in a mesh: grp: 4 (over y, x), dev: 8 (over z, core).
Axes of the slice: x: 2, y: 2, z: 4, core: 2. Of those that a mesh axis runs over, the one named last changes fastest.
Arguments:
- examples: float32 [2048, 32768], P(('grp', 'dev'))
- labels: int32 [2048], P(('grp', 'dev')), may hold values from 0 to 1, as said below
Outputs:
- consensus: float32 [32768], replicated
- local_weights: float32 [32, 32768], P(('grp', 'dev'))
- dual_vars: float32 [32, 32768], P(('grp', 'dev'))
Inputs may be any that keep to these rules, and one draw needn't show every extreme that they name: `labels`: each example's class, 0 or 1.
All inputs are finite; a program needn't handle non-finite values.
Results may differ from a plain program's by a relative error of at most 0.00012.
Values sent between devices are 32-bit elements; how exact they have to be, the bound alone decides.
No kernel may reach another device: no remote copies, remote signals or barrier semaphores. Data moves between devices by JAX's collectives and lax.ppermute only.
A program may use at most 64 MiB of HBM per device.

v0:
```python
import jax
import jax.numpy as jnp
from jax import lax
from jax.sharding import PartitionSpec as P

PROX = 3
ROUNDS = 4


step_size = 200.0
penalty = 0.005
thresh = 0.04


def shrink(values):
    return values - jnp.clip(values, -thresh, thresh)


def local_steps(examples, targets, weight_vector, consensus_point):
    for prox_index in range(PROX):
        label_margins = jnp.dot(examples, weight_vector, precision=lax.Precision.HIGHEST)
        primal_residual = jax.nn.sigmoid(label_margins) - targets
        loss_gradient = jnp.dot(primal_residual, examples, precision=lax.Precision.HIGHEST)
        weight_vector = (
            weight_vector - step_size * loss_gradient + step_size * penalty * consensus_point
        ) / (1.0 + step_size * penalty)
    return weight_vector


def per_device(examples, labels):
    members = lax.axis_size("grp") * lax.axis_size("dev")
    targets = labels.astype(jnp.float32)
    width = examples.shape[1]

    def one_round(round_index, carried):
        consensus, weight_vector, dual_vars = carried
        consensus_point = consensus - dual_vars
        weight_vector = local_steps(examples, targets, weight_vector, consensus_point)
        combined = weight_vector + dual_vars
        summed = lax.psum(combined, ("grp", "dev"))
        consensus = shrink(summed / members)
        dual_vars = dual_vars + weight_vector - consensus
        return (consensus, weight_vector, dual_vars)

    start = (
        jnp.zeros((width,), jnp.float32),
        jnp.zeros((width,), jnp.float32),
        jnp.zeros((width,), jnp.float32),
    )
    consensus, weight_vector, dual_vars = lax.fori_loop(0, ROUNDS, one_round, start)
    return (consensus, weight_vector[None, :], dual_vars[None, :])


def solution(mesh):
    placed = (P(("grp", "dev"), None), P(("grp", "dev")))
    return jax.shard_map(
        per_device,
        mesh=mesh,
        in_specs=placed,
        out_specs=(P(), P(("grp", "dev"), None), P(("grp", "dev"), None)),
        check_vma=False,
    )
```

profile of v0, /device:TPU:0, one launch (start us, length us, event | category | flops | bytes accessed | tf_op | source)
XLA Modules:
  0.0 658.6 jit_solution(14624794344501646285)
XLA Ops:
  7.2 0.7 convert_element_type.3
  7.8 643.4 %while.15 = (s32[]{:T(128)}, f32[32768]{0:T(1024)S(1)}, f32[32768]{0:T(1024)S(1)}, f32[32768]{0:T(1024)S(1)}, f32[64,32768]{1,0:T(8,128)}, /*index=5*/f32[64]{0:T(128)S(1)}, s32[]{:T(128)}, s32[]{:T(128)}) while((s32[]{:T(128)}, f32[32768]{0:T(1024)S(1)}, f32[32768]{0:T(1024)S(1)}, f32[32768]{0:T(1024)S(1)}, ...), condition=%wide.region_2.3_spmd.clone, body=%wide.region_0.2_spmd.clone.sunk | while | flops 151782144 | bytes 88344992 | solution.py:50
  7.8 0.0 all-reduce.2.cloned.1.call-start
  7.8 0.0 copy-start
  7.9 9.1 %fusion.65 = f32[64,1]{0,1:T(1,128)S(1)} fusion(f32[64]{0:T(128)S(1)} %get-tuple-element.149, f32[64,32768]{1,0:T(8,128)} %get-tuple-element.148, f32[32768,1]{0,1:T(1,128)S(1)} %bitcast.118), kind=kOutput, calls=%fused_computation.20.clone.1 | convolution fusion | flops 25166080 | bytes 8520192 | tf_op jit(solution)/shard_map/while/body/eval_jaxpr/dot_general | solution.py:21
  16.9 0.0 copy-done
  16.9 4.0 fusion.66
  21.0 6.6 fusion.67
  27.6 4.1 fusion.68
  31.7 6.6 fusion.69
  38.3 4.1 fusion.70
  42.3 0.7 select_add_fusion.2
  43.0 0.0 all-reduce.2.cloned.1.call-update
  43.0 127.3 %all-reduce.2.cloned.1.call-done = f32[32768]{0:T(1024)} async-done(((f32[32768]{0:T(1024)}), f32[32768]{0:T(1024)}) %all-reduce.2.cloned.1.call-update) | async-done | bytes 131088 | tf_op jit(solution)/shard_map/while/body/eval_jaxpr/psum | solution.py:40
  170.4 1.0 fusion.71
  171.4 0.0 all-reduce.2.cloned.1.call-start
  171.4 0.0 copy-start
  171.5 9.1 %fusion.65 = f32[64,1]{0,1:T(1,128)S(1)} fusion(f32[64]{0:T(128)S(1)} %get-tuple-element.149, f32[64,32768]{1,0:T(8,128)} %get-tuple-element.148, f32[32768,1]{0,1:T(1,128)S(1)} %bitcast.118), kind=kOutput, calls=%fused_computation.20.clone.1 | convolution fusion | flops 25166080 | bytes 8520192 | tf_op jit(solution)/shard_map/while/body/eval_jaxpr/dot_general | solution.py:21
  180.5 0.0 copy-done
  180.5 4.0 fusion.66
  184.6 6.6 fusion.67
  191.2 4.1 fusion.68
  195.3 6.6 fusion.69
  201.9 4.1 fusion.70
  205.9 0.7 select_add_fusion.2
  206.6 0.0 all-reduce.2.cloned.1.call-update
  206.6 123.7 %all-reduce.2.cloned.1.call-done = f32[32768]{0:T(1024)} async-done(((f32[32768]{0:T(1024)}), f32[32768]{0:T(1024)}) %all-reduce.2.cloned.1.call-update) | async-done | bytes 131088 | tf_op jit(solution)/shard_map/while/body/eval_jaxpr/psum | solution.py:40
  330.3 1.0 fusion.71
  331.3 0.0 all-reduce.2.cloned.1.call-start
  331.4 0.0 copy-start
  331.4 9.1 %fusion.65 = f32[64,1]{0,1:T(1,128)S(1)} fusion(f32[64]{0:T(128)S(1)} %get-tuple-element.149, f32[64,32768]{1,0:T(8,128)} %get-tuple-element.148, f32[32768,1]{0,1:T(1,128)S(1)} %bitcast.118), kind=kOutput, calls=%fused_computation.20.clone.1 | convolution fusion | flops 25166080 | bytes 8520192 | tf_op jit(solution)/shard_map/while/body/eval_jaxpr/dot_general | solution.py:21
  340.5 0.0 copy-done
  340.5 4.0 fusion.66
  344.6 6.6 fusion.67
  351.2 4.1 fusion.68
  355.3 6.6 fusion.69
  361.8 4.1 fusion.70
  365.9 0.7 select_add_fusion.2
  366.6 0.0 all-reduce.2.cloned.1.call-update
  366.6 123.7 %all-reduce.2.cloned.1.call-done = f32[32768]{0:T(1024)} async-done(((f32[32768]{0:T(1024)}), f32[32768]{0:T(1024)}) %all-reduce.2.cloned.1.call-update) | async-done | bytes 131088 | tf_op jit(solution)/shard_map/while/body/eval_jaxpr/psum | solution.py:40
  490.3 1.0 fusion.71
  491.3 0.0 all-reduce.2.cloned.1.call-start
  491.4 0.0 copy-start
  491.4 9.1 %fusion.65 = f32[64,1]{0,1:T(1,128)S(1)} fusion(f32[64]{0:T(128)S(1)} %get-tuple-element.149, f32[64,32768]{1,0:T(8,128)} %get-tuple-element.148, f32[32768,1]{0,1:T(1,128)S(1)} %bitcast.118), kind=kOutput, calls=%fused_computation.20.clone.1 | convolution fusion | flops 25166080 | bytes 8520192 | tf_op jit(solution)/shard_map/while/body/eval_jaxpr/dot_general | solution.py:21
  500.5 0.0 copy-done
  500.5 4.0 fusion.66
  504.6 6.6 fusion.67
  511.1 4.1 fusion.68
  515.2 6.6 fusion.69
  521.8 4.1 fusion.70
  525.9 0.7 select_add_fusion.2
  526.6 0.0 all-reduce.2.cloned.1.call-update
  526.6 123.7 %all-reduce.2.cloned.1.call-done = f32[32768]{0:T(1024)} async-done(((f32[32768]{0:T(1024)}), f32[32768]{0:T(1024)}) %all-reduce.2.cloned.1.call-update) | async-done | bytes 131088 | tf_op jit(solution)/shard_map/while/body/eval_jaxpr/psum | solution.py:40
  650.3 1.0 fusion.71
  651.3 0.0 copy-start.1
  651.3 0.0 copy-start.2
  651.3 0.0 copy-start.3
  651.3 0.6 copy-done.1
  651.9 0.0 copy-done.2
  652.0 0.0 copy-done.3
  (15 shorter events, 0.4 us)
Async XLA Ops:
  7.8 162.5 %all-reduce.2.cloned.1.call-start = ((), (), s32[]{:S(2)}) async-start(), calls=%async_computation | async-start | bytes 262144 | tf_op jit(solution)/shard_map/while/body/eval_jaxpr/psum | solution.py:40
  7.8 9.1 %copy-start = (f32[64,32768]{1,0:T(8,128)S(1)}, f32[64,32768]{1,0:T(8,128)}, u32[]{:S(2)}) copy-start(f32[64,32768]{1,0:T(8,128)} %get-tuple-element.148) | copy-start | bytes 25165828 | tf_op jit(solution)/shard_map/while
  171.4 159.0 %all-reduce.2.cloned.1.call-start = ((), (), s32[]{:S(2)}) async-start(), calls=%async_computation | async-start | bytes 262144 | tf_op jit(solution)/shard_map/while/body/eval_jaxpr/psum | solution.py:40
  171.4 9.1 %copy-start = (f32[64,32768]{1,0:T(8,128)S(1)}, f32[64,32768]{1,0:T(8,128)}, u32[]{:S(2)}) copy-start(f32[64,32768]{1,0:T(8,128)} %get-tuple-element.148) | copy-start | bytes 25165828 | tf_op jit(solution)/shard_map/while
  331.3 159.0 %all-reduce.2.cloned.1.call-start = ((), (), s32[]{:S(2)}) async-start(), calls=%async_computation | async-start | bytes 262144 | tf_op jit(solution)/shard_map/while/body/eval_jaxpr/psum | solution.py:40
  331.4 9.1 %copy-start = (f32[64,32768]{1,0:T(8,128)S(1)}, f32[64,32768]{1,0:T(8,128)}, u32[]{:S(2)}) copy-start(f32[64,32768]{1,0:T(8,128)} %get-tuple-element.148) | copy-start | bytes 25165828 | tf_op jit(solution)/shard_map/while
  491.3 159.0 %all-reduce.2.cloned.1.call-start = ((), (), s32[]{:S(2)}) async-start(), calls=%async_computation | async-start | bytes 262144 | tf_op jit(solution)/shard_map/while/body/eval_jaxpr/psum | solution.py:40
  491.4 9.1 %copy-start = (f32[64,32768]{1,0:T(8,128)S(1)}, f32[64,32768]{1,0:T(8,128)}, u32[]{:S(2)}) copy-start(f32[64,32768]{1,0:T(8,128)} %get-tuple-element.148) | copy-start | bytes 25165828 | tf_op jit(solution)/shard_map/while
  651.3 0.7 copy-start.1
  651.3 0.7 copy-start.2
  651.3 0.7 copy-start.3
Sparse Core Ops, SparseCore 0:
  43.2 127.1 all-reduce.1
  206.8 123.5 all-reduce.1
  366.7 123.5 all-reduce.1
  526.7 123.5 all-reduce.1
where the time goes:
time: 659 us
  waiting for transfers between devices  498 us (76%)
  matrix products  137 us (21%)
  between operations  13.7 us (2%)
  other arithmetic  7.74 us (1%)
    psum x4, waiting for transfers between devices, one_round(): summed = lax.psum(combined, ('grp', 'dev'))  498 us
    dot_general x12, matrix products, local_steps(): jnp.dot(examples, weight_vector, precision=lax.Precision.HIGHEST)  88.9 us
    dot_general x12, matrix products, local_steps(): jnp.dot(primal_residual, examples, precision=lax.Precision.HIGHEST)  48.6 us
  transfers between devices with their start and end apart: 4, of which 4 were waited for; matrix products, arithmetic and copies ran while one was open for 0% of the time, Pallas kernels for 0%

commit v1 on v0

v1 whole, which is shorter than its diff:
```python
import functools

import jax
import jax.numpy as jnp
from jax import lax
from jax.experimental import pallas as pl
from jax.experimental.pallas import tpu as pltpu
from jax.sharding import PartitionSpec as P

PROX = 3
ROUNDS = 4

step_size = 200.0
penalty = 0.005
thresh = 0.04

DENOM = 1.0 + step_size * penalty
PULL = step_size * penalty / DENOM
KEEP = 1.0 / DENOM
GRAD = step_size / DENOM
KEEP_ALL = KEEP**PROX
PULL_ALL = PULL * sum(KEEP**s for s in range(PROX))
GRAD_AT = [GRAD * KEEP ** (PROX - 1 - s) for s in range(PROX)]

LANES = 128
SUB = 8
STEP = LANES * SUB
AXES = ("grp", "dev")
F32 = jnp.float32
SCRATCH_BYTES = 8 << 20


def vmem(x):
    return pltpu.with_memory_space_constraint(x, pltpu.VMEM)


def shrink(values):
    return values - jnp.clip(values, -thresh, thresh)


def half_of():
    group = lax.axis_index("grp")
    bits = lax.axis_index("dev")
    for shift in range(max(1, (lax.axis_size("grp") - 1).bit_length())):
        bits = bits + (group >> shift)
    return bits & 1


def column(row):
    rows = row.shape[1]
    eye = lax.broadcasted_iota(jnp.int32, (rows, rows), 0) == lax.broadcasted_iota(jnp.int32, (rows, rows), 1)
    picked = jnp.where(eye, jnp.broadcast_to(row, (rows, rows)), 0.0)
    return jnp.broadcast_to(jnp.sum(picked, axis=1, keepdims=True), (rows, LANES))


def lanes_sum(values):
    return jnp.broadcast_to(jnp.sum(values, axis=1, keepdims=True), values.shape)


def gram_times(gram, residual):
    rows = gram.shape[0]
    row = jnp.sum(gram * residual, axis=0, keepdims=True)
    eye = lax.broadcasted_iota(jnp.int32, gram.shape, 0) == lax.broadcasted_iota(jnp.int32, gram.shape, 1)
    return lanes_sum(jnp.where(eye, jnp.broadcast_to(row, gram.shape), 0.0))


def blocks(x_ref, step):
    for j in range(SUB):
        yield j, x_ref[:, pl.ds(pl.multiple_of(step * STEP + j * LANES, LANES), LANES)]


def times_vector(x_ref, vec_ref, steps):
    def body(step, acc):
        vec = vec_ref[pl.ds(pl.multiple_of(step * SUB, SUB), SUB), :]
        for j, x in blocks(x_ref, step):
            acc = acc + x * vec[j : j + 1, :]
        return acc

    zero = jnp.zeros((x_ref.shape[0], LANES), F32)
    return lanes_sum(lax.fori_loop(0, steps, body, zero, unroll=2))


def transposed_times(x_ref, coef, out_ref, first, steps):
    def body(i, carry):
        rows = [jnp.sum(x * coef, axis=0, keepdims=True) for _, x in blocks(x_ref, first + i)]
        out_ref[pl.ds(pl.multiple_of(i * SUB, SUB), SUB), :] = jnp.concatenate(rows, axis=0)
        return carry

    lax.fori_loop(0, steps, body, 0, unroll=2)


def forth_and_back(x_ref, coef, first, steps, acc):
    def body(i, acc):
        for _, x in blocks(x_ref, first + i):
            acc = acc + x * jnp.sum(x * coef, axis=0, keepdims=True)
        return acc

    return lax.fori_loop(0, steps, body, acc, unroll=2)


def halves_out(x_ref, coef, keep_ref, send_ref, half, steps):
    transposed_times(x_ref, coef, send_ref, (1 - half) * (steps // 2), steps // 2)
    transposed_times(x_ref, coef, keep_ref, half * (steps // 2), steps // 2)


def first_kernel(chunks, steps, x_hbm, label_ref, x_ref, keep_ref, send_ref, coef_ref, target_ref, sems):
    half = half_of()
    rows, width = x_ref.shape
    cols = width // chunks

    def fetch(i):
        span = pl.ds(i * cols, cols)
        return pltpu.make_async_copy(x_hbm.at[:, span], x_ref.at[:, span], sems.at[i])

    for i in range(chunks):
        fetch(i).start()
    target = column(label_ref[...].astype(F32))
    target_ref[...] = target
    residual = 0.5 - target
    coef = GRAD_AT[0] * residual
    acc = jnp.zeros((rows, LANES), F32)
    per = steps // chunks
    for i in range(chunks):
        fetch(i).wait()
        acc = forth_and_back(x_ref, residual, i * per, per, acc)
    margin = -GRAD * lanes_sum(acc)
    for s in range(1, PROX):
        residual = jax.nn.sigmoid(margin) - target
        coef = coef + GRAD_AT[s] * residual
        if s + 1 < PROX:
            acc = forth_and_back(x_ref, residual, 0, steps, jnp.zeros((rows, LANES), F32))
            margin = KEEP * margin - GRAD * lanes_sum(acc)
    coef_ref[...] = coef
    halves_out(x_ref, coef, keep_ref, send_ref, half, steps)


def gram_kernel(steps, x_ref, coef_ref, gram_ref, margin_ref):
    rows = x_ref.shape[0]

    def body(i, acc):
        x = x_ref[:, pl.ds(pl.multiple_of(i * STEP, STEP), STEP)]
        high = x.astype(jnp.bfloat16)
        low = (x - high.astype(F32)).astype(jnp.bfloat16)
        both = jnp.concatenate([high, low], axis=0)
        return acc + lax.dot_general(both, both, (((1,), (1,)), ((), ())), preferred_element_type=F32)

    prod = lax.fori_loop(0, steps, body, jnp.zeros((2 * rows, 2 * rows), F32), unroll=2)
    prod = prod[:rows] + prod[rows:]
    gram = prod + pltpu.roll(prod, rows, 1)
    gram_ref[...] = gram
    margin_ref[...] = -gram_times(gram, coef_ref[...])


def round_kernel(
    steps,
    members,
    x_ref,
    own_ref,
    other_ref,
    z_in,
    u_in,
    w_in,
    gram_ref,
    mw_in,
    mu_in,
    target_ref,
    keep_ref,
    send_ref,
    z_ref,
    u_ref,
    w_ref,
    mw_ref,
    mu_ref,
):
    half = half_of()
    count = own_ref.shape[0]
    for ref, at in ((own_ref, half), (other_ref, 1 - half)):
        span = pl.ds(pl.multiple_of(at * count, count), count)
        u_old = u_in[span, :]
        w_new = KEEP_ALL * w_in[span, :] + PULL_ALL * (z_in[span, :] - u_old) - ref[...] * (1.0 / members)
        average = w_new + u_old
        z_new = shrink(average)
        z_ref[span, :] = z_new
        u_ref[span, :] = average - z_new
        w_ref[span, :] = w_new
    xz = times_vector(x_ref, z_ref, steps)
    gram = gram_ref[...]
    target = target_ref[...]
    margin = mw_in[...]
    mu = mu_in[...] + margin - xz
    mu_ref[...] = mu
    pull = PULL * (xz - mu)
    coef = None
    for s in range(PROX):
        residual = jax.nn.sigmoid(margin) - target
        part = GRAD_AT[s] * residual
        coef = part if coef is None else coef + part
        margin = KEEP * margin + pull - GRAD * gram_times(gram, residual)
    mw_ref[...] = margin
    halves_out(x_ref, coef, keep_ref, send_ref, half, steps)


def last_kernel(members, own_ref, other_ref, z_in, u_in, w_in, sum_ref, z_ref, dual_ref):
    half = half_of()
    count = own_ref.shape[0]
    for ref, at in ((own_ref, half), (other_ref, 1 - half)):
        span = pl.ds(pl.multiple_of(at * count, count), count)
        u_old = u_in[span, :]
        w_new = KEEP_ALL * w_in[span, :] + PULL_ALL * (z_in[span, :] - u_old) - ref[...] * (1.0 / members)
        z_new = shrink(w_new + u_old)
        z_ref[span, :] = z_new
        dual_ref[span, :] = sum_ref[span, :] - z_new


def local_kernel(keep_ref, send_ref, z_ref, u_in, w_in, u_ref, w_ref, both_ref):
    half = half_of()
    count = keep_ref.shape[0]
    for ref, at in ((keep_ref, half), (send_ref, 1 - half)):
        span = pl.ds(pl.multiple_of(at * count, count), count)
        z = z_ref[span, :]
        w_old = w_in[span, :]
        u = u_in[span, :] + w_old - z
        w = KEEP_ALL * w_old + PULL_ALL * (z - u) - ref[...]
        u_ref[span, :] = u
        w_ref[span, :] = w
        both_ref[span, :] = u + w


def exchange(values, mask, members):
    return lax.ppermute(values, AXES, [(i, i ^ mask) for i in range(members)])


def stages(n_grp, n_dev):
    found = []
    bits = [n_dev << b for b in range(n_grp.bit_length() - 1)]
    for i in range(0, len(bits), 2):
        pair = bits[i : i + 2]
        found.append([b | 1 for b in pair] + ([sum(pair)] if len(pair) > 1 else []))
    bits = [1 << b for b in range(1, n_dev.bit_length() - 1)]
    for i in range(0, len(bits), 2):
        pair = bits[i : i + 2]
        found.append(pair[::-1] + ([sum(pair)] if len(pair) > 1 else []))
    return found


def sum_halves(keep, send, n_grp, n_dev):
    members = n_grp * n_dev
    total = keep + exchange(send, 1, members)
    for masks in stages(n_grp, n_dev):
        got = [exchange(total, mask, members) for mask in masks]
        if len(got) == 3:
            total = (total + got[0]) + (got[1] + got[2])
        else:
            total = total + got[0]
    return total, exchange(total, 1, members)


def per_device(examples, labels):
    n_grp, n_dev = lax.axis_size("grp"), lax.axis_size("dev")
    members = n_grp * n_dev
    rows, width = examples.shape
    if n_grp & (n_grp - 1) or n_dev & (n_dev - 1) or n_dev < 2:
        raise ValueError("mesh axes")
    steps = width // STEP
    lines = width // LANES
    chunks = 8
    small = pltpu.VMEM((rows, LANES), F32)
    half = pltpu.VMEM((lines // 2, LANES), F32)
    full = pltpu.VMEM((lines, LANES), F32)
    here = pl.BlockSpec(memory_space=pltpu.VMEM)

    def call(body, outs, n_in, **kw):
        params = pltpu.CompilerParams(vmem_limit_bytes=SCRATCH_BYTES)
        return pl.pallas_call(body, compiler_params=params, out_shape=outs, in_specs=kw.pop("in_specs", [here] * n_in), out_specs=[here] * len(outs), **kw)

    x, keep, send, coef, target = call(
        functools.partial(first_kernel, chunks, steps),
        [pltpu.VMEM((rows, width), F32), half, half, small, small],
        2,
        in_specs=[pl.BlockSpec(memory_space=pltpu.HBM), here],
        scratch_shapes=[pltpu.SemaphoreType.DMA((chunks,))],
        name="first",
    )(pltpu.with_memory_space_constraint(examples, pltpu.HBM), labels.reshape(1, rows))
    gram, mw = call(functools.partial(gram_kernel, steps), [small, small], 2, name="gram")(vmem(x), coef)
    mu = jnp.zeros((rows, LANES), F32)
    z = jnp.zeros((lines, LANES), F32)
    u = z
    w = z

    local_u = local_w = z
    for turn in range(ROUNDS):
        local_u, local_w, both = call(local_kernel, [full, full, full], 5, name="local")(keep, send, z, local_u, local_w)
        own, other = sum_halves(keep, send, n_grp, n_dev)
        if turn + 1 == ROUNDS:
            break
        keep, send, z, u, w, mw, mu = call(
            functools.partial(round_kernel, steps, members),
            [half, half, full, full, full, small, small],
            10,
            name="round",
        )(vmem(x), own, other, z, u, w, gram, mw, mu, target)
    out = jax.ShapeDtypeStruct((lines, LANES), F32)
    z, dual = call(functools.partial(last_kernel, members), [out, out], 6, name="last")(
        own, other, z, u, w, both
    )
    return z.reshape(width), local_w.reshape(1, width), dual.reshape(1, width)


def solution(mesh):
    placed = (P(AXES, None), P(AXES))
    return jax.shard_map(
        per_device,
        mesh=mesh,
        in_specs=placed,
        out_specs=(P(), P(AXES, None), P(AXES, None)),
        check_vma=False,
    )
```

time: 659 us -> 100 us (0.15)
  waiting for transfers between devices: 498 us -> 39.5 us
  matrix products: 137 us -> 0 us
  starting transfers between devices: 0.13 us -> 33.6 us
  Pallas kernels: 0 us -> 24.6 us
  between operations: 13.7 us -> 0.79 us
  other arithmetic: 7.74 us -> 0.17 us
    psum x4 -> x0, waiting for transfers between devices: 498 us -> none  [one_round(): summed = lax.psum(combined, ('grp', 'dev'))]
    dot_general x24 -> x0, matrix products: 137 us -> none  [the longest x12 88.9 us: local_steps(): jnp.dot(examples, weight_vector, precision=lax.Precision.HIGHEST)]
    ppermute x0 -> x32, waiting for transfers between devices: none -> 39.5 us  [exchange(): return lax.ppermute(values, AXES, [(i, i ^ mask) for i in range(members)])]
    ppermute x0 -> x32, starting transfers between devices: none -> 33.6 us  [exchange(): return lax.ppermute(values, AXES, [(i, i ^ mask) for i in range(members)])]
    pallas_call x0 -> x10, Pallas kernels: none -> 24.6 us  [the longest x3 9.32 us: per_device(): call(functools.partial(round_kernel, steps, members), [half, half, full,...]
  transfers between devices with their start and end apart: 4 -> 32, of which waited for: 4 -> 26; matrix products, arithmetic and copies ran while one was open for 0% -> 1% of each run, Pallas kernels for 0% -> 8%
where the time goes in v1:
time: 100 us
  waiting for transfers between devices  39.5 us (40%)
  starting transfers between devices  33.6 us (34%)
  Pallas kernels  24.6 us (25%)
  local copies, waits for them, and re-layouts  1.32 us (1%)
    ppermute x32, waiting for transfers between devices, exchange(): return lax.ppermute(values, AXES, [(i, i ^ mask) for i in range(members)])  39.5 us
    ppermute x32, starting transfers between devices, exchange(): return lax.ppermute(values, AXES, [(i, i ^ mask) for i in range(members)])  33.6 us
    pallas_call x3, Pallas kernels, per_device(): call(functools.partial(round_kernel, steps, members), [half, half, full,...  9.32 us
    pallas_call x1, Pallas kernels, per_device(): call(functools.partial(first_kernel, chunks, steps), [pltpu.VMEM((rows, w...  6.71 us
    pallas_call x1, Pallas kernels, per_device(): call(functools.partial(gram_kernel, steps), [small, small], 2, name='gram')  5.05 us
    pallas_call x4, Pallas kernels, per_device(): call(local_kernel, [full, full, full], 5, name='local')  2.8 us
  transfers between devices with their start and end apart: 32, of which 26 were waited for; matrix products, arithmetic and copies ran while one was open for 1% of the time, Pallas kernels for 8%

profile of v1, /device:TPU:0, one launch (start us, length us, event | category | flops | bytes accessed | tf_op | source)
XLA Modules:
  0.0 100.0 jit_solution(6882834745529782137)
XLA Ops:
  0.6 0.6 copy-done
  1.3 6.7 %first.1 = (f32[64,32768]{1,0:T(8,128)S(1)}, f32[128,128]{1,0:T(8,128)S(1)}, f32[128,128]{1,0:T(8,128)S(1)}, f32[64,128]{1,0:T(8,128)S(1)}, f32[64,128]{1,0:T(8,128)S(1)}) custom-call(f32[64,32768]{1,0:T(8,128)} %x_hbm.1, s32[1,64]{1,0:T(1,128)S(1)} %bitcast.5), custom_call_target="tpu_custom_call" | custom-call | tf_op jit(solution)/shard_map/first/pallas_call | solution.py:276
  8.0 0.6 collective-permute-start
  8.6 0.9 collective-permute-done
  9.5 3.8 %collective-permute-start.3 = (f32[128,128]{1,0:T(8,128)S(1)}, f32[128,128]{1,0:T(8,128)S(1)}, u32[]{:S(2)}, u32[]{:S(2)}) collective-permute-start(f32[128,128]{1,0:T(8,128)S(1)} %add.84), channel_id=1, source_target_pairs={{0,24},{1,25},{2,26},{3,27},{4,28},{5,29},{6,30},{7,31},{8,16},{9,... | collective-permute-start | bytes 196616 | tf_op jit(solution)/shard_map/ppermute | solution.py:230
  13.3 0.4 collective-permute-start.1
  13.7 2.1 %collective-permute-done.3 = f32[128,128]{1,0:T(8,128)S(1)} collective-permute-done((f32[128,128]{1,0:T(8,128)S(1)}, f32[128,128]{1,0:T(8,128)S(1)}, u32[]{:S(2)}, u32[]{:S(2)}) %collective-permute-start.3) | collective-permute-done | bytes 65568 | tf_op jit(solution)/shard_map/ppermute | solution.py:230
  15.8 1.8 %collective-permute-done.2 = f32[128,128]{1,0:T(8,128)S(1)} collective-permute-done((f32[128,128]{1,0:T(8,128)S(1)}, f32[128,128]{1,0:T(8,128)S(1)}, u32[]{:S(2)}, u32[]{:S(2)}) %collective-permute-start.2) | collective-permute-done | bytes 65568 | tf_op jit(solution)/shard_map/ppermute | solution.py:230
  17.7 3.7 %collective-permute-start.6 = (f32[128,128]{1,0:T(8,128)S(1)}, f32[128,128]{1,0:T(8,128)S(1)}, u32[]{:S(2)}, u32[]{:S(2)}) collective-permute-start(f32[128,128]{1,0:T(8,128)S(1)} %add_add_fusion.7), channel_id=1, source_target_pairs={{0,6},{1,7},{2,4},{3,5},{4,2},{5,3},{6,0},{7,1},{8,14},{9,15},{10,... | collective-permute-start | bytes 196616 | tf_op jit(solution)/shard_map/ppermute | solution.py:230
  21.3 0.8 collective-permute-start.4
  22.1 2.4 %collective-permute-done.6 = f32[128,128]{1,0:T(8,128)S(1)} collective-permute-done((f32[128,128]{1,0:T(8,128)S(1)}, f32[128,128]{1,0:T(8,128)S(1)}, u32[]{:S(2)}, u32[]{:S(2)}) %collective-permute-start.6) | collective-permute-done | bytes 65568 | tf_op jit(solution)/shard_map/ppermute | solution.py:230
  24.5 1.9 %collective-permute-done.5 = f32[128,128]{1,0:T(8,128)S(1)} collective-permute-done((f32[128,128]{1,0:T(8,128)S(1)}, f32[128,128]{1,0:T(8,128)S(1)}, u32[]{:S(2)}, u32[]{:S(2)}) %collective-permute-start.5) | collective-permute-done | bytes 65568 | tf_op jit(solution)/shard_map/ppermute | solution.py:230
  26.4 0.8 collective-permute-done.4
  27.2 0.1 collective-permute-start.7
  27.3 5.0 %gram.1 = (f32[64,128]{1,0:T(8,128)S(1)}, f32[64,128]{1,0:T(8,128)S(1)}) custom-call(f32[64,32768]{1,0:T(8,128)S(1)} %get-tuple-element.39.x_ref, f32[64,128]{1,0:T(8,128)S(1)} %get-tuple-element.42.coef_ref), custom_call_target="tpu_custom_call" | custom-call | tf_op jit(solution)/shard_map/gram/pallas_call | solution.py:284
  32.4 2.9 %round.3 = (f32[128,128]{1,0:T(8,128)S(1)}, f32[128,128]{1,0:T(8,128)S(1)}, f32[256,128]{1,0:T(8,128)S(1)}, f32[256,128]{1,0:T(8,128)S(1)}, f32[256,128]{1,0:T(8...) custom-call(f32[64,32768]{1,0:T(8,128)S(1)} %get-tuple-element.39.x_ref, f32[128,128]{1,0:T(8,128)S(1)} %add_add_fusion.6.own_ref, ...), custom_call_target="tpu_custom_call" | custom-call | tf_op jit(solution)/shard_map/round/pallas_call | solution.py:296
  35.3 0.6 collective-permute-start.8
  35.9 0.9 collective-permute-done.8
  36.8 1.9 %collective-permute-start.11 = (f32[128,128]{1,0:T(8,128)S(1)}, f32[128,128]{1,0:T(8,128)S(1)}, u32[]{:S(2)}, u32[]{:S(2)}) collective-permute-start(f32[128,128]{1,0:T(8,128)S(1)} %add.91), channel_id=1, source_target_pairs={{0,24},{1,25},{2,26},{3,27},{4,28},{5,29},{6,30},{7,31},{8,16},{9,... | collective-permute-start | bytes 196616 | tf_op jit(solution)/shard_map/ppermute | solution.py:230
  38.7 0.5 collective-permute-start.10
  39.3 0.8 collective-permute-start.9
  40.1 2.1 %collective-permute-done.11 = f32[128,128]{1,0:T(8,128)S(1)} collective-permute-done((f32[128,128]{1,0:T(8,128)S(1)}, f32[128,128]{1,0:T(8,128)S(1)}, u32[]{:S(2)}, u32[]{:S(2)}) %collective-permute-start.11) | collective-permute-done | bytes 65568 | tf_op jit(solution)/shard_map/ppermute | solution.py:230
  42.1 1.3 %collective-permute-done.10 = f32[128,128]{1,0:T(8,128)S(1)} collective-permute-done((f32[128,128]{1,0:T(8,128)S(1)}, f32[128,128]{1,0:T(8,128)S(1)}, u32[]{:S(2)}, u32[]{:S(2)}) %collective-permute-start.10) | collective-permute-done | bytes 65568 | tf_op jit(solution)/shard_map/ppermute | solution.py:230
  43.5 2.2 %collective-permute-start.14 = (f32[128,128]{1,0:T(8,128)S(1)}, f32[128,128]{1,0:T(8,128)S(1)}, u32[]{:S(2)}, u32[]{:S(2)}) collective-permute-start(f32[128,128]{1,0:T(8,128)S(1)} %add_add_fusion.5), channel_id=1, source_target_pairs={{0,6},{1,7},{2,4},{3,5},{4,2},{5,3},{6,0},{7,1},{8,14},{9,15},{10,... | collective-permute-start | bytes 196616 | tf_op jit(solution)/shard_map/ppermute | solution.py:230
  45.7 0.4 collective-permute-start.13
  46.1 1.9 %collective-permute-start.12 = (f32[128,128]{1,0:T(8,128)S(1)}, f32[128,128]{1,0:T(8,128)S(1)}, u32[]{:S(2)}, u32[]{:S(2)}) collective-permute-start(f32[128,128]{1,0:T(8,128)S(1)} %add_add_fusion.5), channel_id=1, source_target_pairs={{0,4},{1,5},{2,6},{3,7},{4,0},{5,1},{6,2},{7,3},{8,12},{9,13},{10,... | collective-permute-start | bytes 196616 | tf_op jit(solution)/shard_map/ppermute | solution.py:230
  48.0 2.2 %collective-permute-done.14 = f32[128,128]{1,0:T(8,128)S(1)} collective-permute-done((f32[128,128]{1,0:T(8,128)S(1)}, f32[128,128]{1,0:T(8,128)S(1)}, u32[]{:S(2)}, u32[]{:S(2)}) %collective-permute-start.14) | collective-permute-done | bytes 65568 | tf_op jit(solution)/shard_map/ppermute | solution.py:230
  50.2 1.7 %collective-permute-done.13 = f32[128,128]{1,0:T(8,128)S(1)} collective-permute-done((f32[128,128]{1,0:T(8,128)S(1)}, f32[128,128]{1,0:T(8,128)S(1)}, u32[]{:S(2)}, u32[]{:S(2)}) %collective-permute-start.13) | collective-permute-done | bytes 65568 | tf_op jit(solution)/shard_map/ppermute | solution.py:230
  51.9 0.9 collective-permute-done.12
  52.9 0.1 collective-permute-start.15
  52.9 1.2 %collective-permute-done.15.other_ref = f32[128,128]{1,0:T(8,128)S(1)} collective-permute-done((f32[128,128]{1,0:T(8,128)S(1)}, f32[128,128]{1,0:T(8,128)S(1)}, u32[]{:S(2)}, u32[]{:S(2)}) %collective-permute-start.15) | collective-permute-done | bytes 65568 | tf_op jit(solution)/shard_map/ppermute | solution.py:230
  54.2 2.9 %round.4 = (f32[128,128]{1,0:T(8,128)S(1)}, f32[128,128]{1,0:T(8,128)S(1)}, f32[256,128]{1,0:T(8,128)S(1)}, f32[256,128]{1,0:T(8,128)S(1)}, f32[256,128]{1,0:T(8...) custom-call(f32[64,32768]{1,0:T(8,128)S(1)} %get-tuple-element.39.x_ref, f32[128,128]{1,0:T(8,128)S(1)} %add_add_fusion.4.own_ref, ...), custom_call_target="tpu_custom_call" | custom-call | tf_op jit(solution)/shard_map/round/pallas_call | solution.py:296
  57.1 0.2 collective-permute-start.16
  57.3 1.1 %collective-permute-done.16 = f32[128,128]{1,0:T(8,128)S(1)} collective-permute-done((f32[128,128]{1,0:T(8,128)S(1)}, f32[128,128]{1,0:T(8,128)S(1)}, u32[]{:S(2)}, u32[]{:S(2)}) %collective-permute-start.16) | collective-permute-done | bytes 65568 | tf_op jit(solution)/shard_map/ppermute | solution.py:230
  58.4 1.9 %collective-permute-start.19 = (f32[128,128]{1,0:T(8,128)S(1)}, f32[128,128]{1,0:T(8,128)S(1)}, u32[]{:S(2)}, u32[]{:S(2)}) collective-permute-start(f32[128,128]{1,0:T(8,128)S(1)} %add.98), channel_id=1, source_target_pairs={{0,24},{1,25},{2,26},{3,27},{4,28},{5,29},{6,30},{7,31},{8,16},{9,... | collective-permute-start | bytes 196616 | tf_op jit(solution)/shard_map/ppermute | solution.py:230
  60.3 0.3 collective-permute-start.18
  60.7 1.0 collective-permute-start.17
  61.7 2.0 %collective-permute-done.19 = f32[128,128]{1,0:T(8,128)S(1)} collective-permute-done((f32[128,128]{1,0:T(8,128)S(1)}, f32[128,128]{1,0:T(8,128)S(1)}, u32[]{:S(2)}, u32[]{:S(2)}) %collective-permute-start.19) | collective-permute-done | bytes 65568 | tf_op jit(solution)/shard_map/ppermute | solution.py:230
  63.7 1.4 %collective-permute-done.18 = f32[128,128]{1,0:T(8,128)S(1)} collective-permute-done((f32[128,128]{1,0:T(8,128)S(1)}, f32[128,128]{1,0:T(8,128)S(1)}, u32[]{:S(2)}, u32[]{:S(2)}) %collective-permute-start.18) | collective-permute-done | bytes 65568 | tf_op jit(solution)/shard_map/ppermute | solution.py:230
  65.1 2.1 %collective-permute-start.22 = (f32[128,128]{1,0:T(8,128)S(1)}, f32[128,128]{1,0:T(8,128)S(1)}, u32[]{:S(2)}, u32[]{:S(2)}) collective-permute-start(f32[128,128]{1,0:T(8,128)S(1)} %add_add_fusion.3), channel_id=1, source_target_pairs={{0,6},{1,7},{2,4},{3,5},{4,2},{5,3},{6,0},{7,1},{8,14},{9,15},{10,... | collective-permute-start | bytes 196616 | tf_op jit(solution)/shard_map/ppermute | solution.py:230
  67.2 2.3 %collective-permute-start.20 = (f32[128,128]{1,0:T(8,128)S(1)}, f32[128,128]{1,0:T(8,128)S(1)}, u32[]{:S(2)}, u32[]{:S(2)}) collective-permute-start(f32[128,128]{1,0:T(8,128)S(1)} %add_add_fusion.3), channel_id=1, source_target_pairs={{0,4},{1,5},{2,6},{3,7},{4,0},{5,1},{6,2},{7,3},{8,12},{9,13},{10,... | collective-permute-start | bytes 196616 | tf_op jit(solution)/shard_map/ppermute | solution.py:230
  69.5 2.3 %collective-permute-done.22 = f32[128,128]{1,0:T(8,128)S(1)} collective-permute-done((f32[128,128]{1,0:T(8,128)S(1)}, f32[128,128]{1,0:T(8,128)S(1)}, u32[]{:S(2)}, u32[]{:S(2)}) %collective-permute-start.22) | collective-permute-done | bytes 65568 | tf_op jit(solution)/shard_map/ppermute | solution.py:230
  71.9 1.8 %collective-permute-done.21 = f32[128,128]{1,0:T(8,128)S(1)} collective-permute-done((f32[128,128]{1,0:T(8,128)S(1)}, f32[128,128]{1,0:T(8,128)S(1)}, u32[]{:S(2)}, u32[]{:S(2)}) %collective-permute-start.21) | collective-permute-done | bytes 65568 | tf_op jit(solution)/shard_map/ppermute | solution.py:230
  73.7 0.4 collective-permute-done.20
  74.1 1.2 %collective-permute-done.23.other_ref = f32[128,128]{1,0:T(8,128)S(1)} collective-permute-done((f32[128,128]{1,0:T(8,128)S(1)}, f32[128,128]{1,0:T(8,128)S(1)}, u32[]{:S(2)}, u32[]{:S(2)}) %collective-permute-start.23) | collective-permute-done | bytes 65568 | tf_op jit(solution)/shard_map/ppermute | solution.py:230
  75.4 3.5 %round.5 = (f32[128,128]{1,0:T(8,128)S(1)}, f32[128,128]{1,0:T(8,128)S(1)}, f32[256,128]{1,0:T(8,128)S(1)}, f32[256,128]{1,0:T(8,128)S(1)}, f32[256,128]{1,0:T(8...) custom-call(f32[64,32768]{1,0:T(8,128)S(1)} %get-tuple-element.39.x_ref, f32[128,128]{1,0:T(8,128)S(1)} %add_add_fusion.2.own_ref, ...), custom_call_target="tpu_custom_call" | custom-call | tf_op jit(solution)/shard_map/round/pallas_call | solution.py:296
  78.9 0.2 collective-permute-start.24
  79.0 1.1 %collective-permute-done.24 = f32[128,128]{1,0:T(8,128)S(1)} collective-permute-done((f32[128,128]{1,0:T(8,128)S(1)}, f32[128,128]{1,0:T(8,128)S(1)}, u32[]{:S(2)}, u32[]{:S(2)}) %collective-permute-start.24) | collective-permute-done | bytes 65568 | tf_op jit(solution)/shard_map/ppermute | solution.py:230
  80.2 1.8 %collective-permute-start.27 = (f32[128,128]{1,0:T(8,128)S(1)}, f32[128,128]{1,0:T(8,128)S(1)}, u32[]{:S(2)}, u32[]{:S(2)}) collective-permute-start(f32[128,128]{1,0:T(8,128)S(1)} %add.105), channel_id=1, source_target_pairs={{0,24},{1,25},{2,26},{3,27},{4,28},{5,29},{6,30},{7,31},{8,16},{9,... | collective-permute-start | bytes 196616 | tf_op jit(solution)/shard_map/ppermute | solution.py:230
  82.0 0.4 collective-permute-start.26
  82.4 1.1 %collective-permute-start.25 = (f32[128,128]{1,0:T(8,128)S(1)}, f32[128,128]{1,0:T(8,128)S(1)}, u32[]{:S(2)}, u32[]{:S(2)}) collective-permute-start(f32[128,128]{1,0:T(8,128)S(1)} %add.105), channel_id=1, source_target_pairs={{0,9},{1,8},{2,11},{3,10},{4,13},{5,12},{6,15},{7,14},{8,1},{9,0},... | collective-permute-start | bytes 196616 | tf_op jit(solution)/shard_map/ppermute | solution.py:230
  83.4 2.0 %collective-permute-done.27 = f32[128,128]{1,0:T(8,128)S(1)} collective-permute-done((f32[128,128]{1,0:T(8,128)S(1)}, f32[128,128]{1,0:T(8,128)S(1)}, u32[]{:S(2)}, u32[]{:S(2)}) %collective-permute-start.27) | collective-permute-done | bytes 65568 | tf_op jit(solution)/shard_map/ppermute | solution.py:230
  85.4 1.4 %collective-permute-done.26 = f32[128,128]{1,0:T(8,128)S(1)} collective-permute-done((f32[128,128]{1,0:T(8,128)S(1)}, f32[128,128]{1,0:T(8,128)S(1)}, u32[]{:S(2)}, u32[]{:S(2)}) %collective-permute-start.26) | collective-permute-done | bytes 65568 | tf_op jit(solution)/shard_map/ppermute | solution.py:230
  86.8 2.0 %collective-permute-start.30 = (f32[128,128]{1,0:T(8,128)S(1)}, f32[128,128]{1,0:T(8,128)S(1)}, u32[]{:S(2)}, u32[]{:S(2)}) collective-permute-start(f32[128,128]{1,0:T(8,128)S(1)} %add_add_fusion.1), channel_id=1, source_target_pairs={{0,6},{1,7},{2,4},{3,5},{4,2},{5,3},{6,0},{7,1},{8,14},{9,15},{10,... | collective-permute-start | bytes 196616 | tf_op jit(solution)/shard_map/ppermute | solution.py:230
  88.8 2.4 %collective-permute-start.28 = (f32[128,128]{1,0:T(8,128)S(1)}, f32[128,128]{1,0:T(8,128)S(1)}, u32[]{:S(2)}, u32[]{:S(2)}) collective-permute-start(f32[128,128]{1,0:T(8,128)S(1)} %add_add_fusion.1), channel_id=1, source_target_pairs={{0,4},{1,5},{2,6},{3,7},{4,0},{5,1},{6,2},{7,3},{8,12},{9,13},{10,... | collective-permute-start | bytes 196616 | tf_op jit(solution)/shard_map/ppermute | solution.py:230
  91.3 2.5 %collective-permute-done.30 = f32[128,128]{1,0:T(8,128)S(1)} collective-permute-done((f32[128,128]{1,0:T(8,128)S(1)}, f32[128,128]{1,0:T(8,128)S(1)}, u32[]{:S(2)}, u32[]{:S(2)}) %collective-permute-start.30) | collective-permute-done | bytes 65568 | tf_op jit(solution)/shard_map/ppermute | solution.py:230
  93.7 1.7 %collective-permute-done.29 = f32[128,128]{1,0:T(8,128)S(1)} collective-permute-done((f32[128,128]{1,0:T(8,128)S(1)}, f32[128,128]{1,0:T(8,128)S(1)}, u32[]{:S(2)}, u32[]{:S(2)}) %collective-permute-start.29) | collective-permute-done | bytes 65568 | tf_op jit(solution)/shard_map/ppermute | solution.py:230
  95.4 0.3 collective-permute-done.28
  95.8 0.7 local.4
  96.5 0.7 local.5
  97.2 0.7 local.6
  97.9 0.7 local.7
  98.6 0.7 copy.5
  99.2 0.8 last.1
  (27 shorter events, 0.4 us)
Async XLA Ops:
  0.6 0.7 copy-start
  8.0 1.5 %collective-permute-start = (f32[128,128]{1,0:T(8,128)S(1)}, f32[128,128]{1,0:T(8,128)S(1)}, u32[]{:S(2)}, u32[]{:S(2)}) collective-permute-start(f32[128,128]{1,0:T(8,128)S(1)} %get-tuple-element.41.send_ref), channel_id=1, source_target_pairs={{0,1},{1,0},{2,3},{3,2},{4,5},{5,4},{6,7},{7,6},{8,9},{9,8},{10,11... | collective-permute-start | bytes 196616 | tf_op jit(solution)/shard_map/ppermute | solution.py:230
  9.5 6.3 %collective-permute-start.3 = (f32[128,128]{1,0:T(8,128)S(1)}, f32[128,128]{1,0:T(8,128)S(1)}, u32[]{:S(2)}, u32[]{:S(2)}) collective-permute-start(f32[128,128]{1,0:T(8,128)S(1)} %add.84), channel_id=1, source_target_pairs={{0,24},{1,25},{2,26},{3,27},{4,28},{5,29},{6,30},{7,31},{8,16},{9,... | collective-permute-start | bytes 196616 | tf_op jit(solution)/shard_map/ppermute | solution.py:230
  13.3 4.3 %collective-permute-start.2 = (f32[128,128]{1,0:T(8,128)S(1)}, f32[128,128]{1,0:T(8,128)S(1)}, u32[]{:S(2)}, u32[]{:S(2)}) collective-permute-start(f32[128,128]{1,0:T(8,128)S(1)} %add.84), channel_id=1, source_target_pairs={{0,17},{1,16},{2,19},{3,18},{4,21},{5,20},{6,23},{7,22},{8,25},{9,... | collective-permute-start | bytes 196616 | tf_op jit(solution)/shard_map/ppermute | solution.py:230
  13.3 4.3 %collective-permute-start.1 = (f32[128,128]{1,0:T(8,128)S(1)}, f32[128,128]{1,0:T(8,128)S(1)}, u32[]{:S(2)}, u32[]{:S(2)}) collective-permute-start(f32[128,128]{1,0:T(8,128)S(1)} %add.84), channel_id=1, source_target_pairs={{0,9},{1,8},{2,11},{3,10},{4,13},{5,12},{6,15},{7,14},{8,1},{9,0},... | collective-permute-start | bytes 196616 | tf_op jit(solution)/shard_map/ppermute | solution.py:230
  17.7 6.8 %collective-permute-start.6 = (f32[128,128]{1,0:T(8,128)S(1)}, f32[128,128]{1,0:T(8,128)S(1)}, u32[]{:S(2)}, u32[]{:S(2)}) collective-permute-start(f32[128,128]{1,0:T(8,128)S(1)} %add_add_fusion.7), channel_id=1, source_target_pairs={{0,6},{1,7},{2,4},{3,5},{4,2},{5,3},{6,0},{7,1},{8,14},{9,15},{10,... | collective-permute-start | bytes 196616 | tf_op jit(solution)/shard_map/ppermute | solution.py:230
  21.3 5.1 %collective-permute-start.5 = (f32[128,128]{1,0:T(8,128)S(1)}, f32[128,128]{1,0:T(8,128)S(1)}, u32[]{:S(2)}, u32[]{:S(2)}) collective-permute-start(f32[128,128]{1,0:T(8,128)S(1)} %add_add_fusion.7), channel_id=1, source_target_pairs={{0,2},{1,3},{2,0},{3,1},{4,6},{5,7},{6,4},{7,5},{8,10},{9,11},{10,... | collective-permute-start | bytes 196616 | tf_op jit(solution)/shard_map/ppermute | solution.py:230
  21.3 5.9 %collective-permute-start.4 = (f32[128,128]{1,0:T(8,128)S(1)}, f32[128,128]{1,0:T(8,128)S(1)}, u32[]{:S(2)}, u32[]{:S(2)}) collective-permute-start(f32[128,128]{1,0:T(8,128)S(1)} %add_add_fusion.7), channel_id=1, source_target_pairs={{0,4},{1,5},{2,6},{3,7},{4,0},{5,1},{6,2},{7,3},{8,12},{9,13},{10,... | collective-permute-start | bytes 196616 | tf_op jit(solution)/shard_map/ppermute | solution.py:230
  27.2 5.1 %collective-permute-start.7 = (f32[128,128]{1,0:T(8,128)S(1)}, f32[128,128]{1,0:T(8,128)S(1)}, u32[]{:S(2)}, u32[]{:S(2)}) collective-permute-start(f32[128,128]{1,0:T(8,128)S(1)} %add_add_fusion.6.own_ref), channel_id=1, source_target_pairs={{0,1},{1,0},{2,3},{3,2},{4,5},{5,4},{6,7},{7,6},{8,9},{9,8},{10,11... | collective-permute-start | bytes 196616 | tf_op jit(solution)/shard_map/ppermute | solution.py:230
  35.3 1.5 %collective-permute-start.8 = (f32[128,128]{1,0:T(8,128)S(1)}, f32[128,128]{1,0:T(8,128)S(1)}, u32[]{:S(2)}, u32[]{:S(2)}) collective-permute-start(f32[128,128]{1,0:T(8,128)S(1)} %get-tuple-element.47.send_ref), channel_id=1, source_target_pairs={{0,1},{1,0},{2,3},{3,2},{4,5},{5,4},{6,7},{7,6},{8,9},{9,8},{10,11... | collective-permute-start | bytes 196616 | tf_op jit(solution)/shard_map/ppermute | solution.py:230
  36.8 5.4 %collective-permute-start.11 = (f32[128,128]{1,0:T(8,128)S(1)}, f32[128,128]{1,0:T(8,128)S(1)}, u32[]{:S(2)}, u32[]{:S(2)}) collective-permute-start(f32[128,128]{1,0:T(8,128)S(1)} %add.91), channel_id=1, source_target_pairs={{0,24},{1,25},{2,26},{3,27},{4,28},{5,29},{6,30},{7,31},{8,16},{9,... | collective-permute-start | bytes 196616 | tf_op jit(solution)/shard_map/ppermute | solution.py:230
  38.7 4.8 %collective-permute-start.10 = (f32[128,128]{1,0:T(8,128)S(1)}, f32[128,128]{1,0:T(8,128)S(1)}, u32[]{:S(2)}, u32[]{:S(2)}) collective-permute-start(f32[128,128]{1,0:T(8,128)S(1)} %add.91), channel_id=1, source_target_pairs={{0,17},{1,16},{2,19},{3,18},{4,21},{5,20},{6,23},{7,22},{8,25},{9,... | collective-permute-start | bytes 196616 | tf_op jit(solution)/shard_map/ppermute | solution.py:230
  39.3 4.2 %collective-permute-start.9 = (f32[128,128]{1,0:T(8,128)S(1)}, f32[128,128]{1,0:T(8,128)S(1)}, u32[]{:S(2)}, u32[]{:S(2)}) collective-permute-start(f32[128,128]{1,0:T(8,128)S(1)} %add.91), channel_id=1, source_target_pairs={{0,9},{1,8},{2,11},{3,10},{4,13},{5,12},{6,15},{7,14},{8,1},{9,0},... | collective-permute-start | bytes 196616 | tf_op jit(solution)/shard_map/ppermute | solution.py:230
  43.5 6.7 %collective-permute-start.14 = (f32[128,128]{1,0:T(8,128)S(1)}, f32[128,128]{1,0:T(8,128)S(1)}, u32[]{:S(2)}, u32[]{:S(2)}) collective-permute-start(f32[128,128]{1,0:T(8,128)S(1)} %add_add_fusion.5), channel_id=1, source_target_pairs={{0,6},{1,7},{2,4},{3,5},{4,2},{5,3},{6,0},{7,1},{8,14},{9,15},{10,... | collective-permute-start | bytes 196616 | tf_op jit(solution)/shard_map/ppermute | solution.py:230
  45.7 6.2 %collective-permute-start.13 = (f32[128,128]{1,0:T(8,128)S(1)}, f32[128,128]{1,0:T(8,128)S(1)}, u32[]{:S(2)}, u32[]{:S(2)}) collective-permute-start(f32[128,128]{1,0:T(8,128)S(1)} %add_add_fusion.5), channel_id=1, source_target_pairs={{0,2},{1,3},{2,0},{3,1},{4,6},{5,7},{6,4},{7,5},{8,10},{9,11},{10,... | collective-permute-start | bytes 196616 | tf_op jit(solution)/shard_map/ppermute | solution.py:230
  46.1 6.7 %collective-permute-start.12 = (f32[128,128]{1,0:T(8,128)S(1)}, f32[128,128]{1,0:T(8,128)S(1)}, u32[]{:S(2)}, u32[]{:S(2)}) collective-permute-start(f32[128,128]{1,0:T(8,128)S(1)} %add_add_fusion.5), channel_id=1, source_target_pairs={{0,4},{1,5},{2,6},{3,7},{4,0},{5,1},{6,2},{7,3},{8,12},{9,13},{10,... | collective-permute-start | bytes 196616 | tf_op jit(solution)/shard_map/ppermute | solution.py:230
  52.9 1.3 %collective-permute-start.15 = (f32[128,128]{1,0:T(8,128)S(1)}, f32[128,128]{1,0:T(8,128)S(1)}, u32[]{:S(2)}, u32[]{:S(2)}) collective-permute-start(f32[128,128]{1,0:T(8,128)S(1)} %add_add_fusion.4.own_ref), channel_id=1, source_target_pairs={{0,1},{1,0},{2,3},{3,2},{4,5},{5,4},{6,7},{7,6},{8,9},{9,8},{10,11... | collective-permute-start | bytes 196616 | tf_op jit(solution)/shard_map/ppermute | solution.py:230
  57.1 1.3 %collective-permute-start.16 = (f32[128,128]{1,0:T(8,128)S(1)}, f32[128,128]{1,0:T(8,128)S(1)}, u32[]{:S(2)}, u32[]{:S(2)}) collective-permute-start(f32[128,128]{1,0:T(8,128)S(1)} %get-tuple-element.54.send_ref), channel_id=1, source_target_pairs={{0,1},{1,0},{2,3},{3,2},{4,5},{5,4},{6,7},{7,6},{8,9},{9,8},{10,11... | collective-permute-start | bytes 196616 | tf_op jit(solution)/shard_map/ppermute | solution.py:230
  58.4 5.3 %collective-permute-start.19 = (f32[128,128]{1,0:T(8,128)S(1)}, f32[128,128]{1,0:T(8,128)S(1)}, u32[]{:S(2)}, u32[]{:S(2)}) collective-permute-start(f32[128,128]{1,0:T(8,128)S(1)} %add.98), channel_id=1, source_target_pairs={{0,24},{1,25},{2,26},{3,27},{4,28},{5,29},{6,30},{7,31},{8,16},{9,... | collective-permute-start | bytes 196616 | tf_op jit(solution)/shard_map/ppermute | solution.py:230
  60.3 4.7 %collective-permute-start.18 = (f32[128,128]{1,0:T(8,128)S(1)}, f32[128,128]{1,0:T(8,128)S(1)}, u32[]{:S(2)}, u32[]{:S(2)}) collective-permute-start(f32[128,128]{1,0:T(8,128)S(1)} %add.98), channel_id=1, source_target_pairs={{0,17},{1,16},{2,19},{3,18},{4,21},{5,20},{6,23},{7,22},{8,25},{9,... | collective-permute-start | bytes 196616 | tf_op jit(solution)/shard_map/ppermute | solution.py:230
  60.7 4.4 %collective-permute-start.17 = (f32[128,128]{1,0:T(8,128)S(1)}, f32[128,128]{1,0:T(8,128)S(1)}, u32[]{:S(2)}, u32[]{:S(2)}) collective-permute-start(f32[128,128]{1,0:T(8,128)S(1)} %add.98), channel_id=1, source_target_pairs={{0,9},{1,8},{2,11},{3,10},{4,13},{5,12},{6,15},{7,14},{8,1},{9,0},... | collective-permute-start | bytes 196616 | tf_op jit(solution)/shard_map/ppermute | solution.py:230
  65.1 6.8 %collective-permute-start.22 = (f32[128,128]{1,0:T(8,128)S(1)}, f32[128,128]{1,0:T(8,128)S(1)}, u32[]{:S(2)}, u32[]{:S(2)}) collective-permute-start(f32[128,128]{1,0:T(8,128)S(1)} %add_add_fusion.3), channel_id=1, source_target_pairs={{0,6},{1,7},{2,4},{3,5},{4,2},{5,3},{6,0},{7,1},{8,14},{9,15},{10,... | collective-permute-start | bytes 196616 | tf_op jit(solution)/shard_map/ppermute | solution.py:230
  67.2 6.5 %collective-permute-start.21 = (f32[128,128]{1,0:T(8,128)S(1)}, f32[128,128]{1,0:T(8,128)S(1)}, u32[]{:S(2)}, u32[]{:S(2)}) collective-permute-start(f32[128,128]{1,0:T(8,128)S(1)} %add_add_fusion.3), channel_id=1, source_target_pairs={{0,2},{1,3},{2,0},{3,1},{4,6},{5,7},{6,4},{7,5},{8,10},{9,11},{10,... | collective-permute-start | bytes 196616 | tf_op jit(solution)/shard_map/ppermute | solution.py:230
  67.2 6.8 %collective-permute-start.20 = (f32[128,128]{1,0:T(8,128)S(1)}, f32[128,128]{1,0:T(8,128)S(1)}, u32[]{:S(2)}, u32[]{:S(2)}) collective-permute-start(f32[128,128]{1,0:T(8,128)S(1)} %add_add_fusion.3), channel_id=1, source_target_pairs={{0,4},{1,5},{2,6},{3,7},{4,0},{5,1},{6,2},{7,3},{8,12},{9,13},{10,... | collective-permute-start | bytes 196616 | tf_op jit(solution)/shard_map/ppermute | solution.py:230
  74.0 1.3 %collective-permute-start.23 = (f32[128,128]{1,0:T(8,128)S(1)}, f32[128,128]{1,0:T(8,128)S(1)}, u32[]{:S(2)}, u32[]{:S(2)}) collective-permute-start(f32[128,128]{1,0:T(8,128)S(1)} %add_add_fusion.2.own_ref), channel_id=1, source_target_pairs={{0,1},{1,0},{2,3},{3,2},{4,5},{5,4},{6,7},{7,6},{8,9},{9,8},{10,11... | collective-permute-start | bytes 196616 | tf_op jit(solution)/shard_map/ppermute | solution.py:230
  78.9 1.3 %collective-permute-start.24 = (f32[128,128]{1,0:T(8,128)S(1)}, f32[128,128]{1,0:T(8,128)S(1)}, u32[]{:S(2)}, u32[]{:S(2)}) collective-permute-start(f32[128,128]{1,0:T(8,128)S(1)} %get-tuple-element.61.send_ref), channel_id=1, source_target_pairs={{0,1},{1,0},{2,3},{3,2},{4,5},{5,4},{6,7},{7,6},{8,9},{9,8},{10,11... | collective-permute-start | bytes 196616 | tf_op jit(solution)/shard_map/ppermute | solution.py:230
  80.2 5.3 %collective-permute-start.27 = (f32[128,128]{1,0:T(8,128)S(1)}, f32[128,128]{1,0:T(8,128)S(1)}, u32[]{:S(2)}, u32[]{:S(2)}) collective-permute-start(f32[128,128]{1,0:T(8,128)S(1)} %add.105), channel_id=1, source_target_pairs={{0,24},{1,25},{2,26},{3,27},{4,28},{5,29},{6,30},{7,31},{8,16},{9,... | collective-permute-start | bytes 196616 | tf_op jit(solution)/shard_map/ppermute | solution.py:230
  82.0 4.8 %collective-permute-start.26 = (f32[128,128]{1,0:T(8,128)S(1)}, f32[128,128]{1,0:T(8,128)S(1)}, u32[]{:S(2)}, u32[]{:S(2)}) collective-permute-start(f32[128,128]{1,0:T(8,128)S(1)} %add.105), channel_id=1, source_target_pairs={{0,17},{1,16},{2,19},{3,18},{4,21},{5,20},{6,23},{7,22},{8,25},{9,... | collective-permute-start | bytes 196616 | tf_op jit(solution)/shard_map/ppermute | solution.py:230
  82.4 4.4 %collective-permute-start.25 = (f32[128,128]{1,0:T(8,128)S(1)}, f32[128,128]{1,0:T(8,128)S(1)}, u32[]{:S(2)}, u32[]{:S(2)}) collective-permute-start(f32[128,128]{1,0:T(8,128)S(1)} %add.105), channel_id=1, source_target_pairs={{0,9},{1,8},{2,11},{3,10},{4,13},{5,12},{6,15},{7,14},{8,1},{9,0},... | collective-permute-start | bytes 196616 | tf_op jit(solution)/shard_map/ppermute | solution.py:230
  86.8 6.9 %collective-permute-start.30 = (f32[128,128]{1,0:T(8,128)S(1)}, f32[128,128]{1,0:T(8,128)S(1)}, u32[]{:S(2)}, u32[]{:S(2)}) collective-permute-start(f32[128,128]{1,0:T(8,128)S(1)} %add_add_fusion.1), channel_id=1, source_target_pairs={{0,6},{1,7},{2,4},{3,5},{4,2},{5,3},{6,0},{7,1},{8,14},{9,15},{10,... | collective-permute-start | bytes 196616 | tf_op jit(solution)/shard_map/ppermute | solution.py:230
  88.8 6.6 %collective-permute-start.29 = (f32[128,128]{1,0:T(8,128)S(1)}, f32[128,128]{1,0:T(8,128)S(1)}, u32[]{:S(2)}, u32[]{:S(2)}) collective-permute-start(f32[128,128]{1,0:T(8,128)S(1)} %add_add_fusion.1), channel_id=1, source_target_pairs={{0,2},{1,3},{2,0},{3,1},{4,6},{5,7},{6,4},{7,5},{8,10},{9,11},{10,... | collective-permute-start | bytes 196616 | tf_op jit(solution)/shard_map/ppermute | solution.py:230
  88.8 6.8 %collective-permute-start.28 = (f32[128,128]{1,0:T(8,128)S(1)}, f32[128,128]{1,0:T(8,128)S(1)}, u32[]{:S(2)}, u32[]{:S(2)}) collective-permute-start(f32[128,128]{1,0:T(8,128)S(1)} %add_add_fusion.1), channel_id=1, source_target_pairs={{0,4},{1,5},{2,6},{3,7},{4,0},{5,1},{6,2},{7,3},{8,12},{9,13},{10,... | collective-permute-start | bytes 196616 | tf_op jit(solution)/shard_map/ppermute | solution.py:230
  95.7 3.5 %collective-permute-start.31 = (f32[128,128]{1,0:T(8,128)S(1)}, f32[128,128]{1,0:T(8,128)S(1)}, u32[]{:S(2)}, u32[]{:S(2)}) collective-permute-start(f32[128,128]{1,0:T(8,128)S(1)} %add_add_fusion.own_ref), channel_id=1, source_target_pairs={{0,1},{1,0},{2,3},{3,2},{4,5},{5,4},{6,7},{7,6},{8,9},{9,8},{10,11... | collective-permute-start | bytes 196616 | tf_op jit(solution)/shard_map/ppermute | solution.py:230

commit v2 on v0

v2 whole, which is shorter than its diff:
```python
import functools

import jax
import jax.numpy as jnp
from jax import lax
from jax.experimental import pallas as pl
from jax.experimental.pallas import tpu as pltpu
from jax.sharding import PartitionSpec as P


PROX = 3
ROUNDS = 4

step_size = 200.0
penalty = 0.005
thresh = 0.04

DENOM = 1.0 + step_size * penalty
PULL = step_size * penalty / DENOM
KEEP = 1.0 / DENOM
GRAD = step_size / DENOM
KEEP_ALL = KEEP**PROX
PULL_ALL = PULL * sum(KEEP**s for s in range(PROX))
GRAD_AT = [GRAD * KEEP ** (PROX - 1 - s) for s in range(PROX)]

LANES = 128
SUB = 8
AXES = ("grp", "dev")
F32 = jnp.float32
SCRATCH_BYTES = 8 << 20


def vmem(x):
    return pltpu.with_memory_space_constraint(x, pltpu.VMEM)


def shrink(values):
    return values - jnp.clip(values, -thresh, thresh)


def half_of():
    group = lax.axis_index("grp")
    bits = lax.axis_index("dev")
    for shift in range(max(1, (lax.axis_size("grp") - 1).bit_length())):
        bits = bits + (group >> shift)
    return bits & 1


def eye_mask(shape):
    return lax.broadcasted_iota(jnp.int32, shape, 0) == lax.broadcasted_iota(jnp.int32, shape, 1)


def column(row):
    rows = row.shape[1]
    picked = jnp.where(eye_mask((rows, rows)), jnp.broadcast_to(row, (rows, rows)), 0.0)
    return jnp.broadcast_to(jnp.sum(picked, axis=1, keepdims=True), (rows, LANES))


def lanes_sum(values):
    return jnp.broadcast_to(jnp.sum(values, axis=1, keepdims=True), values.shape)


def gram_times(gram, residual):
    row = jnp.sum(gram * residual, axis=0, keepdims=True)
    return lanes_sum(jnp.where(eye_mask(gram.shape), jnp.broadcast_to(row, gram.shape), 0.0))


def strip(i):
    return pl.ds(pl.multiple_of(i * SUB, SUB), SUB)


def times_vector(refs, vec_ref):
    def body(i, accs):
        vec = vec_ref[strip(i), :]
        accs = list(accs)
        for j in range(SUB):
            for n, ref in enumerate(refs):
                accs[n] = accs[n] + ref[i * SUB + j] * vec[j : j + 1, :]
        return tuple(accs)

    zero = jnp.zeros(refs[0].shape[1:], F32)
    return lax.fori_loop(0, refs[0].shape[0] // SUB, body, (zero,) * len(refs))


def transposed_times(pairs, out_ref):
    def body(i, carry):
        rows = []
        for j in range(SUB):
            terms = [ref[i * SUB + j] * coef for ref, coef in pairs]
            rows.append(jnp.sum(functools.reduce(jnp.add, terms), axis=0, keepdims=True))
        out_ref[strip(i), :] = jnp.concatenate(rows, axis=0)
        return carry

    lax.fori_loop(0, out_ref.shape[0] // SUB, body, 0, unroll=2)


def forth_and_back(ref, first, count, coef, acc):
    def body(i, acc):
        for j in range(SUB):
            x = ref[first + i * SUB + j]
            acc = acc + x * jnp.sum(x * coef, axis=0, keepdims=True)
        return acc

    return lax.fori_loop(0, count // SUB, body, acc, unroll=2)


def first_kernel(chunks, x_hbm, label_ref, keep_x, send_x, keep_ref, send_ref, coef_ref, target_ref, sems):
    half = half_of()
    count, rows, _ = keep_x.shape
    tiles = rows // SUB
    per = count // chunks

    def fetch(n, i, t):
        ref, at = ((keep_x, half), (send_x, 1 - half))[n]
        return pltpu.make_async_copy(
            x_hbm.at[t, pl.ds(at * count + i * per, per)],
            ref.at[pl.ds(i * per, per), pl.ds(t * SUB, SUB)],
            sems.at[n, i, t],
        )

    places = [(n, i) for n in range(2) for i in range(chunks)]
    for n, i in places:
        for t in range(tiles):
            fetch(n, i, t).start()
    target = column(label_ref[...].astype(F32))
    target_ref[...] = target
    residual = 0.5 - target
    coef = GRAD_AT[0] * residual
    zero = jnp.zeros((rows, LANES), F32)
    acc = zero
    for n, i in places:
        for t in range(tiles):
            fetch(n, i, t).wait()
        acc = forth_and_back((keep_x, send_x)[n], i * per, per, residual, acc)
    margin = -GRAD * lanes_sum(acc)
    for s in range(1, PROX):
        residual = jax.nn.sigmoid(margin) - target
        coef = coef + GRAD_AT[s] * residual
        if s + 1 < PROX:
            acc = forth_and_back(keep_x, 0, count, residual, zero)
            acc = forth_and_back(send_x, 0, count, residual, acc)
            margin = KEEP * margin - GRAD * lanes_sum(acc)
    coef_ref[...] = coef
    transposed_times([(send_x, coef)], send_ref)
    transposed_times([(keep_x, coef)], keep_ref)


def gram_kernel(keep_x, send_x, coef_ref, target_ref, pack_ref):
    count, rows, _ = keep_x.shape

    def body(i, acc):
        for ref in (keep_x, send_x):
            for j in range(0, SUB, 2):
                x = jnp.concatenate([ref[i * SUB + j], ref[i * SUB + j + 1]], axis=1)
                high = x.astype(jnp.bfloat16)
                low = (x - high.astype(F32)).astype(jnp.bfloat16)
                both = jnp.concatenate([high, low], axis=0)
                acc = acc + lax.dot_general(both, both, (((1,), (1,)), ((), ())), preferred_element_type=F32)
        return acc

    prod = lax.fori_loop(0, count // SUB, body, jnp.zeros((2 * rows, 2 * rows), F32))
    prod = prod[:rows] + prod[rows:]
    gram = prod + pltpu.roll(prod, rows, 1)
    pack_ref[:rows] = gram
    pack_ref[rows : 2 * rows] = -gram_times(gram, coef_ref[...])
    pack_ref[2 * rows :] = target_ref[...]


def point_kernel(members, keep_x, other_x, sum_ref, z_in, u_in, w_in, z_ref, u_ref, w_ref, part_ref):
    rows = keep_x.shape[1]
    u_old = u_in[...]
    w_new = KEEP_ALL * w_in[...] + PULL_ALL * (z_in[...] - u_old) - sum_ref[...] * (1.0 / members)
    average = w_new + u_old
    z_new = shrink(average)
    z_ref[...] = z_new
    u_ref[...] = average - z_new
    w_ref[...] = w_new
    mine, others = times_vector([keep_x, other_x], z_ref)
    part_ref[:rows] = mine
    part_ref[rows:] = others


def prox_kernel(fresh, keep_x, other_x, part_ref, got_ref, own_pack, other_pack, state_in, out_ref, coef_ref, state_ref=None):
    rows = keep_x.shape[1]
    part = part_ref[...]
    got = got_ref[...]
    whole = [part[:rows] + got[rows:], part[rows:] + got[:rows]]
    coefs = []
    for n, pack in enumerate((own_pack, other_pack)):
        at = pl.ds(n * rows, rows)
        mu_at = pl.ds((2 + n) * rows, rows)
        xz = lanes_sum(whole[n])
        gram = pack[:rows]
        target = pack[2 * rows :]
        if fresh:
            margin = pack[rows : 2 * rows]
            mu = margin - xz
        else:
            margin = state_in[at]
            mu = state_in[mu_at] + margin - xz
        pull = PULL * (xz - mu)
        coef = None
        for s in range(PROX):
            residual = jax.nn.sigmoid(margin) - target
            term = GRAD_AT[s] * residual
            coef = term if coef is None else coef + term
            margin = KEEP * margin + pull - GRAD * gram_times(gram, residual)
        if state_ref is not None:
            state_ref[at] = margin
            state_ref[mu_at] = mu
        coefs.append(coef)
    coef_ref[...] = coefs[0]
    transposed_times([(keep_x, coefs[0]), (other_x, coefs[1])], out_ref)


def affine_kernel(u_mean, w_mean, *refs):
    z_refs, out_ref = refs[:-1], refs[-1]
    count = u_mean.shape[0]
    w = u = z = jnp.zeros((count, LANES), F32)
    for z_ref in z_refs:
        w = KEEP_ALL * w + PULL_ALL * (z - u)
        z = z_ref[...]
        u = u + w - z
    w = KEEP_ALL * w + PULL_ALL * (z - u)
    out_ref[:count] = w
    out_ref[count : 2 * count] = u + w
    mean = u_mean[...]
    out_ref[2 * count :] = KEEP_ALL * w_mean[...] + PULL_ALL * (z - mean) + mean


def local_kernel(keep_x, send_x, own_ref, other_ref, *refs):
    coef_refs, (w_ref, both_ref) = refs[:-2], refs[-2:]
    half = half_of()
    count, rows, _ = keep_x.shape
    cw = cu = jnp.zeros((rows, LANES), F32)
    for coef_ref in coef_refs:
        cw = KEEP_ALL * cw - PULL_ALL * cu + coef_ref[...]
        cs = cu + cw
        cu = cs
    for x_ref, z_ref, at in ((keep_x, own_ref, half), (send_x, other_ref, 1 - half)):

        def body(i, carry, x_ref=x_ref, z_ref=z_ref, at=at):
            rows_w, rows_s = [], []
            for j in range(SUB):
                x = x_ref[i * SUB + j]
                rows_w.append(jnp.sum(x * cw, axis=0, keepdims=True))
                rows_s.append(jnp.sum(x * cs, axis=0, keepdims=True))
            to = strip(at * (count // SUB) + i)
            w_ref[to, :] = z_ref[strip(i), :] - jnp.concatenate(rows_w, axis=0)
            both_ref[to, :] = z_ref[strip(count // SUB + i), :] - jnp.concatenate(rows_s, axis=0)
            return carry

        lax.fori_loop(0, count // SUB, body, 0)


def last_kernel(members, own_ref, other_ref, own_base, other_base, both_ref, z_ref, dual_ref):
    half = half_of()
    count = own_ref.shape[0]
    for ref, base, at in ((own_ref, own_base, half), (other_ref, other_base, 1 - half)):
        span = pl.ds(pl.multiple_of(at * count, count), count)
        z_new = shrink(base[2 * count :] - ref[...] * (1.0 / members))
        z_ref[span, :] = z_new
        dual_ref[span, :] = both_ref[span, :] - z_new


def exchange(values, mask):
    members = lax.axis_size("grp") * lax.axis_size("dev")
    return lax.ppermute(values, AXES, [(i, i ^ mask) for i in range(members)])


def stages(n_grp, n_dev):
    found = []
    bits = [n_dev << b for b in range(n_grp.bit_length() - 1)]
    for i in range(0, len(bits), 2):
        pair = bits[i : i + 2]
        found.append([b | 1 for b in pair] + ([sum(pair)] if len(pair) > 1 else []))
    bits = [1 << b for b in range(1, n_dev.bit_length() - 1)]
    for i in range(0, len(bits), 2):
        pair = bits[i : i + 2]
        found.append(pair[::-1] + ([sum(pair)] if len(pair) > 1 else []))
    return found


def sum_chips(total, n_grp, n_dev):
    plan = stages(n_grp, n_dev)
    for masks in plan:
        got = [exchange(total, mask) for mask in masks]
        if len(got) == 3:
            total = (total + got[0]) + (got[1] + got[2])
        else:
            total = total + got[0]
    return total


def call(body, outs, n_in, **kw):
    here = pl.BlockSpec(memory_space=pltpu.VMEM)
    params = pltpu.CompilerParams(vmem_limit_bytes=SCRATCH_BYTES)
    specs = kw.pop("in_specs", [here] * n_in)
    return pl.pallas_call(body, compiler_params=params, out_shape=outs, in_specs=specs, out_specs=[here] * len(outs), **kw)


def per_device(examples, labels):
    n_grp, n_dev = lax.axis_size("grp"), lax.axis_size("dev")
    members = n_grp * n_dev
    rows, width = examples.shape
    if n_grp & (n_grp - 1) or n_dev & (n_dev - 1) or n_dev < 2:
        raise ValueError("mesh axes")
    blocks = width // LANES
    count = blocks // 2
    tiles = rows // SUB
    chunks = 4
    small = pltpu.VMEM((rows, LANES), F32)
    double = pltpu.VMEM((2 * rows, LANES), F32)
    half = pltpu.VMEM((count, LANES), F32)
    x_half = pltpu.VMEM((count, rows, LANES), F32)
    out = jax.ShapeDtypeStruct((blocks, LANES), F32)

    tiled = examples.reshape(tiles, SUB, blocks, LANES).transpose(0, 2, 1, 3)
    keep_x, send_x, keep, send, coef, target = call(
        functools.partial(first_kernel, chunks),
        [x_half, x_half, half, half, small, small],
        2,
        in_specs=[pl.BlockSpec(memory_space=pltpu.HBM), pl.BlockSpec(memory_space=pltpu.VMEM)],
        scratch_shapes=[pltpu.SemaphoreType.DMA((2, chunks, tiles))],
        name="first",
    )(pltpu.with_memory_space_constraint(tiled, pltpu.HBM), labels.reshape(1, rows))
    keep_x = vmem(keep_x)
    send_x = vmem(send_x)
    got = exchange(send, 1)
    got, moved = lax.optimization_barrier((got, send_x))
    other_x = vmem(exchange(moved, 1))
    total = keep + got
    (own_pack,) = call(gram_kernel, [pltpu.VMEM((3 * rows, LANES), F32)], 4, name="gram")(keep_x, send_x, coef, target)
    other_pack = exchange(own_pack, 1)
    z = u = w = jnp.zeros((count, LANES), F32)
    state = [jnp.zeros((4 * rows, LANES), F32)]
    coefs = [coef]
    points = []
    for turn in range(1, ROUNDS):
        total = sum_chips(total, n_grp, n_dev)
        z, u, w, part = call(functools.partial(point_kernel, members), [half, half, half, double], 6, name="point")(
            keep_x, other_x, total, z, u, w
        )
        points.append(z)
        got = exchange(part, 1)
        kept = [pltpu.VMEM((4 * rows, LANES), F32)] if turn + 1 < ROUNDS else []
        total, coef, *state = call(functools.partial(prox_kernel, turn == 1), [half, small, *kept], 7, name="prox")(
            keep_x, other_x, part, got, own_pack, other_pack, *state
        )
        coefs.append(coef)
    (own_base,) = call(affine_kernel, [pltpu.VMEM((3 * count, LANES), F32)], 2 + len(points), name="affine")(u, w, *points)
    other_base = exchange(own_base, 1)
    local_w, both = call(local_kernel, [out, pltpu.VMEM((blocks, LANES), F32)], 4 + len(coefs), name="local")(
        keep_x, send_x, own_base, other_base, *coefs
    )
    total = sum_chips(total, n_grp, n_dev)
    z, dual = call(functools.partial(last_kernel, members), [out, out], 5, name="last")(
        total, exchange(total, 1), own_base, other_base, both
    )
    return z.reshape(width), local_w.reshape(1, width), dual.reshape(1, width)


def solution(mesh):
    placed = (P(AXES, None), P(AXES))
    return jax.shard_map(
        per_device,
        mesh=mesh,
        in_specs=placed,
        out_specs=(P(), P(AXES, None), P(AXES, None)),
        check_vma=False,
    )
```

time: 659 us -> 87.8 us (0.13)
  waiting for transfers between devices: 498 us -> 32.6 us
  matrix products: 137 us -> 0 us
  starting transfers between devices: 0.13 us -> 33.4 us
  Pallas kernels: 0 us -> 20 us
  between operations: 13.7 us -> 0.83 us
  other arithmetic: 7.74 us -> 0.15 us
    psum x4 -> x0, waiting for transfers between devices: 498 us -> none  [one_round(): summed = lax.psum(combined, ('grp', 'dev'))]
    dot_general x24 -> x0, matrix products: 137 us -> none  [the longest x12 88.9 us: local_steps(): jnp.dot(examples, weight_vector, precision=lax.Precision.HIGHEST)]
    ppermute x0 -> x32, starting transfers between devices: none -> 33.4 us  [exchange(): return lax.ppermute(values, AXES, [(i, i ^ mask) for i in range(members)])]
    ppermute x0 -> x32, waiting for transfers between devices: none -> 32.6 us  [exchange(): return lax.ppermute(values, AXES, [(i, i ^ mask) for i in range(members)])]
    pallas_call x0 -> x11, Pallas kernels: none -> 20 us  [the longest x1 6.59 us: per_device(): call(functools.partial(first_kernel, chunks), [x_half, x_half, half, half...]
  transfers between devices with their start and end apart: 4 -> 32, of which waited for: 4 -> 21; matrix products, arithmetic and copies ran while one was open for 0% -> 0% of each run, Pallas kernels for 0% -> 9%
where the time goes in v2:
time: 87.8 us; the launch traced here: 87.6 us
  starting transfers between devices  33.4 us (38%)
  waiting for transfers between devices  32.6 us (37%)
  Pallas kernels  20 us (23%)
    ppermute x32, starting transfers between devices, exchange(): return lax.ppermute(values, AXES, [(i, i ^ mask) for i in range(members)])  33.4 us
    ppermute x32, waiting for transfers between devices, exchange(): return lax.ppermute(values, AXES, [(i, i ^ mask) for i in range(members)])  32.6 us
    pallas_call x1, Pallas kernels, per_device(): call(functools.partial(first_kernel, chunks), [x_half, x_half, half, half...  6.59 us
    pallas_call x1, Pallas kernels, per_device(): call(gram_kernel, [pltpu.VMEM((3 * rows, LANES), F32)], 4, name='gram')  5.01 us
    pallas_call x3, Pallas kernels, per_device(): call(functools.partial(prox_kernel, turn == 1), [half, small, *kept], 7,...  3.1 us
    pallas_call x1, Pallas kernels, per_device(): call(local_kernel, [out, pltpu.VMEM((blocks, LANES), F32)], 4 + len(coefs...  2.52 us
    pallas_call x3, Pallas kernels, per_device(): call(functools.partial(point_kernel, members), [half, half, half, double]...  2 us
  transfers between devices with their start and end apart: 32, of which 21 were waited for; matrix products, arithmetic and copies ran while one was open for 0% of the time, Pallas kernels for 9%

profile of v2, /device:TPU:0, one launch (start us, length us, event | category | flops | bytes accessed | tf_op | source)
XLA Modules:
  0.0 87.6 jit_solution(12611594390330873101)
XLA Ops:
  0.6 0.6 copy-done
  1.3 6.6 %first.1 = (f32[128,64,128]{2,1,0:T(8,128)S(1)}, f32[128,64,128]{2,1,0:T(8,128)S(1)}, f32[128,128]{1,0:T(8,128)S(1)}, f32[128,128]{1,0:T(8,128)S(1)}, f32[64,128]{1,0:T(8,128)S(1)}, /*index=5*/f32[64,128]{1,0:T(8,128)S(1)}) custom-call(f32[8,256,8,128]{3,2,1,0:T(8,128)} %bitcast.8, s32[1,64]{1,0:T(1,128)S(1)} %bitcast.7), custom_call_target="tpu_custom_call" | custom-call | tf_op jit(solution)/shard_map/first/pallas_call | solution.py:319
  7.9 0.6 collective-permute-start
  8.4 0.9 %collective-permute-done = f32[128,128]{1,0:T(8,128)S(1)} collective-permute-done((f32[128,128]{1,0:T(8,128)S(1)}, f32[128,128]{1,0:T(8,128)S(1)}, u32[]{:S(2)}, u32[]{:S(2)}) %collective-permute-start) | collective-permute-done | bytes 65568 | tf_op jit(solution)/shard_map/ppermute | solution.py:268
  9.3 0.4 collective-permute-start.1
  9.7 3.7 %collective-permute-start.4 = (f32[128,128]{1,0:T(8,128)S(1)}, f32[128,128]{1,0:T(8,128)S(1)}, u32[]{:S(2)}, u32[]{:S(2)}) collective-permute-start(f32[128,128]{1,0:T(8,128)S(1)} %add.75), channel_id=1, source_target_pairs={{0,24},{1,25},{2,26},{3,27},{4,28},{5,29},{6,30},{7,31},{8,16},{9,... | collective-permute-start | bytes 196616 | tf_op jit(solution)/shard_map/ppermute | solution.py:268
  13.4 0.2 collective-permute-start.3
  13.5 0.2 collective-permute-start.2
  13.7 2.2 %collective-permute-done.4 = f32[128,128]{1,0:T(8,128)S(1)} collective-permute-done((f32[128,128]{1,0:T(8,128)S(1)}, f32[128,128]{1,0:T(8,128)S(1)}, u32[]{:S(2)}, u32[]{:S(2)}) %collective-permute-start.4) | collective-permute-done | bytes 65568 | tf_op jit(solution)/shard_map/ppermute | solution.py:268
  16.0 1.5 %collective-permute-done.3 = f32[128,128]{1,0:T(8,128)S(1)} collective-permute-done((f32[128,128]{1,0:T(8,128)S(1)}, f32[128,128]{1,0:T(8,128)S(1)}, u32[]{:S(2)}, u32[]{:S(2)}) %collective-permute-start.3) | collective-permute-done | bytes 65568 | tf_op jit(solution)/shard_map/ppermute | solution.py:268
  17.5 0.0 collective-permute-done.2
  17.5 3.7 %collective-permute-start.7 = (f32[128,128]{1,0:T(8,128)S(1)}, f32[128,128]{1,0:T(8,128)S(1)}, u32[]{:S(2)}, u32[]{:S(2)}) collective-permute-start(f32[128,128]{1,0:T(8,128)S(1)} %add_add_fusion.7), channel_id=1, source_target_pairs={{0,6},{1,7},{2,4},{3,5},{4,2},{5,3},{6,0},{7,1},{8,14},{9,15},{10,... | collective-permute-start | bytes 196616 | tf_op jit(solution)/shard_map/ppermute | solution.py:268
  21.2 0.0 collective-permute-start.6
  21.2 0.8 collective-permute-start.5
  22.0 5.0 %gram.1.own_pack = f32[192,128]{1,0:T(8,128)S(1)} custom-call(f32[128,64,128]{2,1,0:T(8,128)S(1)} %get-tuple-element.35.keep_x, f32[128,64,128]{2,1,0:T(8,128)S(1)} %get-tuple-element.38.send_x, f32[64,128]{1,0:T(8,128)S(1)} %get-tuple-element.42.coef_ref.refs_0_, f32[64,128]{1,0:T(8,128)S(1)} %get-tuple-element.43.target_ref), custom_call_target="tpu_custom_call" | custom-call | tf_op jit(solution)/shard_map/gram/pallas_call | solution.py:333
  27.0 0.0 collective-permute-start.9
  27.0 0.0 collective-permute-done.5
  27.1 0.7 point.3
  27.8 0.5 collective-permute-start.8
  28.3 0.9 %collective-permute-done.8.got_ref = f32[128,128]{1,0:T(8,128)S(1)} collective-permute-done((f32[128,128]{1,0:T(8,128)S(1)}, f32[128,128]{1,0:T(8,128)S(1)}, u32[]{:S(2)}, u32[]{:S(2)}) %collective-permute-start.8) | collective-permute-done | bytes 65568 | tf_op jit(solution)/shard_map/ppermute | solution.py:268
  29.2 1.1 %prox.3 = (f32[128,128]{1,0:T(8,128)S(1)}, f32[64,128]{1,0:T(8,128)S(1)}, f32[256,128]{1,0:T(8,128)S(1)}) custom-call(f32[128,64,128]{2,1,0:T(8,128)S(1)} %get-tuple-element.35.keep_x, f32[128,64,128]{2,1,0:T(8,128)S(1)} %collective-permute-done.1.other_x, f32[128,128]{1,0:T(8,128)S(1)} %get-tuple-element.41.part_ref, ...), custom_call_target="tpu_custom_call" | custom-call | tf_op jit(solution)/shard_map/prox/pallas_call | solution.py:347
  30.3 1.8 %collective-permute-start.12 = (f32[128,128]{1,0:T(8,128)S(1)}, f32[128,128]{1,0:T(8,128)S(1)}, u32[]{:S(2)}, u32[]{:S(2)}) collective-permute-start(f32[128,128]{1,0:T(8,128)S(1)} %get-tuple-element.44), channel_id=1, source_target_pairs={{0,24},{1,25},{2,26},{3,27},{4,28},{5,29},{6,30},{7,31},{8,16},{9,... | collective-permute-start | bytes 196616 | tf_op jit(solution)/shard_map/ppermute | solution.py:268
  32.1 0.9 %collective-permute-start.11 = (f32[128,128]{1,0:T(8,128)S(1)}, f32[128,128]{1,0:T(8,128)S(1)}, u32[]{:S(2)}, u32[]{:S(2)}) collective-permute-start(f32[128,128]{1,0:T(8,128)S(1)} %get-tuple-element.44), channel_id=1, source_target_pairs={{0,17},{1,16},{2,19},{3,18},{4,21},{5,20},{6,23},{7,22},{8,25},{9,... | collective-permute-start | bytes 196616 | tf_op jit(solution)/shard_map/ppermute | solution.py:268
  33.0 0.5 collective-permute-start.10
  33.6 2.1 %collective-permute-done.12 = f32[128,128]{1,0:T(8,128)S(1)} collective-permute-done((f32[128,128]{1,0:T(8,128)S(1)}, f32[128,128]{1,0:T(8,128)S(1)}, u32[]{:S(2)}, u32[]{:S(2)}) %collective-permute-start.12) | collective-permute-done | bytes 65568 | tf_op jit(solution)/shard_map/ppermute | solution.py:268
  35.7 1.3 %collective-permute-done.11 = f32[128,128]{1,0:T(8,128)S(1)} collective-permute-done((f32[128,128]{1,0:T(8,128)S(1)}, f32[128,128]{1,0:T(8,128)S(1)}, u32[]{:S(2)}, u32[]{:S(2)}) %collective-permute-start.11) | collective-permute-done | bytes 65568 | tf_op jit(solution)/shard_map/ppermute | solution.py:268
  37.0 3.7 %collective-permute-start.15 = (f32[128,128]{1,0:T(8,128)S(1)}, f32[128,128]{1,0:T(8,128)S(1)}, u32[]{:S(2)}, u32[]{:S(2)}) collective-permute-start(f32[128,128]{1,0:T(8,128)S(1)} %add_add_fusion.5), channel_id=1, source_target_pairs={{0,6},{1,7},{2,4},{3,5},{4,2},{5,3},{6,0},{7,1},{8,14},{9,15},{10,... | collective-permute-start | bytes 196616 | tf_op jit(solution)/shard_map/ppermute | solution.py:268
  40.7 0.8 collective-permute-start.13
  41.5 2.4 %collective-permute-done.15 = f32[128,128]{1,0:T(8,128)S(1)} collective-permute-done((f32[128,128]{1,0:T(8,128)S(1)}, f32[128,128]{1,0:T(8,128)S(1)}, u32[]{:S(2)}, u32[]{:S(2)}) %collective-permute-start.15) | collective-permute-done | bytes 65568 | tf_op jit(solution)/shard_map/ppermute | solution.py:268
  43.9 2.1 %collective-permute-done.14 = f32[128,128]{1,0:T(8,128)S(1)} collective-permute-done((f32[128,128]{1,0:T(8,128)S(1)}, f32[128,128]{1,0:T(8,128)S(1)}, u32[]{:S(2)}, u32[]{:S(2)}) %collective-permute-start.14) | collective-permute-done | bytes 65568 | tf_op jit(solution)/shard_map/ppermute | solution.py:268
  46.0 0.6 collective-permute-done.13
  46.6 0.7 point.4
  47.3 0.1 collective-permute-start.16
  47.3 1.2 %collective-permute-done.16.got_ref = f32[128,128]{1,0:T(8,128)S(1)} collective-permute-done((f32[128,128]{1,0:T(8,128)S(1)}, f32[128,128]{1,0:T(8,128)S(1)}, u32[]{:S(2)}, u32[]{:S(2)}) %collective-permute-start.16) | collective-permute-done | bytes 65568 | tf_op jit(solution)/shard_map/ppermute | solution.py:268
  48.6 1.1 %prox.4 = (f32[128,128]{1,0:T(8,128)S(1)}, f32[64,128]{1,0:T(8,128)S(1)}, f32[256,128]{1,0:T(8,128)S(1)}) custom-call(f32[128,64,128]{2,1,0:T(8,128)S(1)} %get-tuple-element.35.keep_x, f32[128,64,128]{2,1,0:T(8,128)S(1)} %collective-permute-done.1.other_x, f32[128,128]{1,0:T(8,128)S(1)} %get-tuple-element.48.part_ref, ...), custom_call_target="tpu_custom_call" | custom-call | tf_op jit(solution)/shard_map/prox/pallas_call | solution.py:347
  49.7 2.0 %collective-permute-start.19 = (f32[128,128]{1,0:T(8,128)S(1)}, f32[128,128]{1,0:T(8,128)S(1)}, u32[]{:S(2)}, u32[]{:S(2)}) collective-permute-start(f32[128,128]{1,0:T(8,128)S(1)} %get-tuple-element.50), channel_id=1, source_target_pairs={{0,24},{1,25},{2,26},{3,27},{4,28},{5,29},{6,30},{7,31},{8,16},{9,... | collective-permute-start | bytes 196616 | tf_op jit(solution)/shard_map/ppermute | solution.py:268
  51.6 0.6 collective-permute-start.18
  52.2 0.7 collective-permute-start.17
  52.9 2.0 %collective-permute-done.19 = f32[128,128]{1,0:T(8,128)S(1)} collective-permute-done((f32[128,128]{1,0:T(8,128)S(1)}, f32[128,128]{1,0:T(8,128)S(1)}, u32[]{:S(2)}, u32[]{:S(2)}) %collective-permute-start.19) | collective-permute-done | bytes 65568 | tf_op jit(solution)/shard_map/ppermute | solution.py:268
  54.9 1.4 %collective-permute-done.18 = f32[128,128]{1,0:T(8,128)S(1)} collective-permute-done((f32[128,128]{1,0:T(8,128)S(1)}, f32[128,128]{1,0:T(8,128)S(1)}, u32[]{:S(2)}, u32[]{:S(2)}) %collective-permute-start.18) | collective-permute-done | bytes 65568 | tf_op jit(solution)/shard_map/ppermute | solution.py:268
  56.3 2.4 %collective-permute-start.22 = (f32[128,128]{1,0:T(8,128)S(1)}, f32[128,128]{1,0:T(8,128)S(1)}, u32[]{:S(2)}, u32[]{:S(2)}) collective-permute-start(f32[128,128]{1,0:T(8,128)S(1)} %add_add_fusion.3), channel_id=1, source_target_pairs={{0,6},{1,7},{2,4},{3,5},{4,2},{5,3},{6,0},{7,1},{8,14},{9,15},{10,... | collective-permute-start | bytes 196616 | tf_op jit(solution)/shard_map/ppermute | solution.py:268
  58.7 0.4 collective-permute-start.21
  59.0 1.7 %collective-permute-start.20 = (f32[128,128]{1,0:T(8,128)S(1)}, f32[128,128]{1,0:T(8,128)S(1)}, u32[]{:S(2)}, u32[]{:S(2)}) collective-permute-start(f32[128,128]{1,0:T(8,128)S(1)} %add_add_fusion.3), channel_id=1, source_target_pairs={{0,4},{1,5},{2,6},{3,7},{4,0},{5,1},{6,2},{7,3},{8,12},{9,13},{10,... | collective-permute-start | bytes 196616 | tf_op jit(solution)/shard_map/ppermute | solution.py:268
  60.8 2.4 %collective-permute-done.22 = f32[128,128]{1,0:T(8,128)S(1)} collective-permute-done((f32[128,128]{1,0:T(8,128)S(1)}, f32[128,128]{1,0:T(8,128)S(1)}, u32[]{:S(2)}, u32[]{:S(2)}) %collective-permute-start.22) | collective-permute-done | bytes 65568 | tf_op jit(solution)/shard_map/ppermute | solution.py:268
  63.1 1.9 %collective-permute-done.21 = f32[128,128]{1,0:T(8,128)S(1)} collective-permute-done((f32[128,128]{1,0:T(8,128)S(1)}, f32[128,128]{1,0:T(8,128)S(1)}, u32[]{:S(2)}, u32[]{:S(2)}) %collective-permute-start.21) | collective-permute-done | bytes 65568 | tf_op jit(solution)/shard_map/ppermute | solution.py:268
  65.0 0.6 collective-permute-done.20
  65.6 0.7 point.5
  66.3 0.1 collective-permute-start.23
  66.4 1.2 %collective-permute-done.23.got_ref = f32[128,128]{1,0:T(8,128)S(1)} collective-permute-done((f32[128,128]{1,0:T(8,128)S(1)}, f32[128,128]{1,0:T(8,128)S(1)}, u32[]{:S(2)}, u32[]{:S(2)}) %collective-permute-start.23) | collective-permute-done | bytes 65568 | tf_op jit(solution)/shard_map/ppermute | solution.py:268
  67.6 1.0 %prox.5 = (f32[128,128]{1,0:T(8,128)S(1)}, f32[64,128]{1,0:T(8,128)S(1)}) custom-call(f32[128,64,128]{2,1,0:T(8,128)S(1)} %get-tuple-element.35.keep_x, f32[128,64,128]{2,1,0:T(8,128)S(1)} %collective-permute-done.1.other_x, f32[128,128]{1,0:T(8,128)S(1)} %get-tuple-element.54.part_ref, f32[128,128]{1,0:T(8,128)S(1)} %collective-permute-done.23.got_ref, ...), custom_call_target="tpu_custom_call" | custom-call | tf_op jit(solution)/shard_map/prox/pallas_call | solution.py:347
  68.6 1.8 %collective-permute-start.26 = (f32[128,128]{1,0:T(8,128)S(1)}, f32[128,128]{1,0:T(8,128)S(1)}, u32[]{:S(2)}, u32[]{:S(2)}) collective-permute-start(f32[128,128]{1,0:T(8,128)S(1)} %get-tuple-element.56), channel_id=1, source_target_pairs={{0,24},{1,25},{2,26},{3,27},{4,28},{5,29},{6,30},{7,31},{8,16},{9,... | collective-permute-start | bytes 196616 | tf_op jit(solution)/shard_map/ppermute | solution.py:268
  70.4 0.7 collective-permute-start.25
  71.1 0.7 collective-permute-start.24
  71.9 2.0 %collective-permute-done.26 = f32[128,128]{1,0:T(8,128)S(1)} collective-permute-done((f32[128,128]{1,0:T(8,128)S(1)}, f32[128,128]{1,0:T(8,128)S(1)}, u32[]{:S(2)}, u32[]{:S(2)}) %collective-permute-start.26) | collective-permute-done | bytes 65568 | tf_op jit(solution)/shard_map/ppermute | solution.py:268
  73.9 1.4 %collective-permute-done.25 = f32[128,128]{1,0:T(8,128)S(1)} collective-permute-done((f32[128,128]{1,0:T(8,128)S(1)}, f32[128,128]{1,0:T(8,128)S(1)}, u32[]{:S(2)}, u32[]{:S(2)}) %collective-permute-start.25) | collective-permute-done | bytes 65568 | tf_op jit(solution)/shard_map/ppermute | solution.py:268
  75.2 2.3 %collective-permute-start.29 = (f32[128,128]{1,0:T(8,128)S(1)}, f32[128,128]{1,0:T(8,128)S(1)}, u32[]{:S(2)}, u32[]{:S(2)}) collective-permute-start(f32[128,128]{1,0:T(8,128)S(1)} %add_add_fusion.1), channel_id=1, source_target_pairs={{0,6},{1,7},{2,4},{3,5},{4,2},{5,3},{6,0},{7,1},{8,14},{9,15},{10,... | collective-permute-start | bytes 196616 | tf_op jit(solution)/shard_map/ppermute | solution.py:268
  77.6 2.1 %collective-permute-start.27 = (f32[128,128]{1,0:T(8,128)S(1)}, f32[128,128]{1,0:T(8,128)S(1)}, u32[]{:S(2)}, u32[]{:S(2)}) collective-permute-start(f32[128,128]{1,0:T(8,128)S(1)} %add_add_fusion.1), channel_id=1, source_target_pairs={{0,4},{1,5},{2,6},{3,7},{4,0},{5,1},{6,2},{7,3},{8,12},{9,13},{10,... | collective-permute-start | bytes 196616 | tf_op jit(solution)/shard_map/ppermute | solution.py:268
  79.7 0.1 collective-permute-start.31
  79.8 2.3 %collective-permute-done.29 = f32[128,128]{1,0:T(8,128)S(1)} collective-permute-done((f32[128,128]{1,0:T(8,128)S(1)}, f32[128,128]{1,0:T(8,128)S(1)}, u32[]{:S(2)}, u32[]{:S(2)}) %collective-permute-start.29) | collective-permute-done | bytes 65568 | tf_op jit(solution)/shard_map/ppermute | solution.py:268
  82.2 1.9 %collective-permute-done.28 = f32[128,128]{1,0:T(8,128)S(1)} collective-permute-done((f32[128,128]{1,0:T(8,128)S(1)}, f32[128,128]{1,0:T(8,128)S(1)}, u32[]{:S(2)}, u32[]{:S(2)}) %collective-permute-start.28) | collective-permute-done | bytes 65568 | tf_op jit(solution)/shard_map/ppermute | solution.py:268
  84.1 0.2 collective-permute-done.27
  84.3 0.1 collective-permute-start.30
  84.4 2.5 %local.1 = (f32[256,128]{1,0:T(8,128)}, f32[256,128]{1,0:T(8,128)S(1)}) custom-call(f32[128,64,128]{2,1,0:T(8,128)S(1)} %get-tuple-element.35.keep_x, f32[128,64,128]{2,1,0:T(8,128)S(1)} %get-tuple-element.38.send_x, f32[384,128]{1,0:T(8,128)S(1)} %affine.1.own_ref.own_base, f32[384,128]{1,0:T(8,128)S(1)} %collective-permute-done.31.other_ref.other_base, ...), custom_call_target="tpu_custom_call" | custom-call | tf_op jit(solution)/shard_map/local/pallas_call | solution.py:353
  86.9 0.7 last.1
  (24 shorter events, 0.2 us)
Async XLA Ops:
  0.6 0.7 copy-start
  7.9 1.5 %collective-permute-start = (f32[128,128]{1,0:T(8,128)S(1)}, f32[128,128]{1,0:T(8,128)S(1)}, u32[]{:S(2)}, u32[]{:S(2)}) collective-permute-start(f32[128,128]{1,0:T(8,128)S(1)} %get-tuple-element.36), channel_id=1, source_target_pairs={{0,1},{1,0},{2,3},{3,2},{4,5},{5,4},{6,7},{7,6},{8,9},{9,8},{10,11... | collective-permute-start | bytes 196616 | tf_op jit(solution)/shard_map/ppermute | solution.py:268
  9.3 17.7 %collective-permute-start.1 = (f32[128,64,128]{2,1,0:T(8,128)S(1)}, f32[128,64,128]{2,1,0:T(8,128)S(1)}, u32[]{:S(2)}, u32[]{:S(2)}) collective-permute-start(f32[128,64,128]{2,1,0:T(8,128)S(1)} %get-tuple-element.38.send_x), channel_id=1, source_target_pairs={{0,1},{1,0},{2,3},{3,2},{4,5},{5,4},{6,7},{7,6},{8,9},{9,8},{10,11... | collective-permute-start | bytes 12582920 | tf_op jit(solution)/shard_map/ppermute | solution.py:268
  9.7 6.3 %collective-permute-start.4 = (f32[128,128]{1,0:T(8,128)S(1)}, f32[128,128]{1,0:T(8,128)S(1)}, u32[]{:S(2)}, u32[]{:S(2)}) collective-permute-start(f32[128,128]{1,0:T(8,128)S(1)} %add.75), channel_id=1, source_target_pairs={{0,24},{1,25},{2,26},{3,27},{4,28},{5,29},{6,30},{7,31},{8,16},{9,... | collective-permute-start | bytes 196616 | tf_op jit(solution)/shard_map/ppermute | solution.py:268
  13.4 4.1 %collective-permute-start.3 = (f32[128,128]{1,0:T(8,128)S(1)}, f32[128,128]{1,0:T(8,128)S(1)}, u32[]{:S(2)}, u32[]{:S(2)}) collective-permute-start(f32[128,128]{1,0:T(8,128)S(1)} %add.75), channel_id=1, source_target_pairs={{0,17},{1,16},{2,19},{3,18},{4,21},{5,20},{6,23},{7,22},{8,25},{9,... | collective-permute-start | bytes 196616 | tf_op jit(solution)/shard_map/ppermute | solution.py:268
  13.5 4.0 %collective-permute-start.2 = (f32[128,128]{1,0:T(8,128)S(1)}, f32[128,128]{1,0:T(8,128)S(1)}, u32[]{:S(2)}, u32[]{:S(2)}) collective-permute-start(f32[128,128]{1,0:T(8,128)S(1)} %add.75), channel_id=1, source_target_pairs={{0,9},{1,8},{2,11},{3,10},{4,13},{5,12},{6,15},{7,14},{8,1},{9,0},... | collective-permute-start | bytes 196616 | tf_op jit(solution)/shard_map/ppermute | solution.py:268
  17.5 9.5 %collective-permute-start.7 = (f32[128,128]{1,0:T(8,128)S(1)}, f32[128,128]{1,0:T(8,128)S(1)}, u32[]{:S(2)}, u32[]{:S(2)}) collective-permute-start(f32[128,128]{1,0:T(8,128)S(1)} %add_add_fusion.7), channel_id=1, source_target_pairs={{0,6},{1,7},{2,4},{3,5},{4,2},{5,3},{6,0},{7,1},{8,14},{9,15},{10,... | collective-permute-start | bytes 196616 | tf_op jit(solution)/shard_map/ppermute | solution.py:268
  21.2 5.8 %collective-permute-start.6 = (f32[128,128]{1,0:T(8,128)S(1)}, f32[128,128]{1,0:T(8,128)S(1)}, u32[]{:S(2)}, u32[]{:S(2)}) collective-permute-start(f32[128,128]{1,0:T(8,128)S(1)} %add_add_fusion.7), channel_id=1, source_target_pairs={{0,2},{1,3},{2,0},{3,1},{4,6},{5,7},{6,4},{7,5},{8,10},{9,11},{10,... | collective-permute-start | bytes 196616 | tf_op jit(solution)/shard_map/ppermute | solution.py:268
  21.2 5.9 %collective-permute-start.5 = (f32[128,128]{1,0:T(8,128)S(1)}, f32[128,128]{1,0:T(8,128)S(1)}, u32[]{:S(2)}, u32[]{:S(2)}) collective-permute-start(f32[128,128]{1,0:T(8,128)S(1)} %add_add_fusion.7), channel_id=1, source_target_pairs={{0,4},{1,5},{2,6},{3,7},{4,0},{5,1},{6,2},{7,3},{8,12},{9,13},{10,... | collective-permute-start | bytes 196616 | tf_op jit(solution)/shard_map/ppermute | solution.py:268
  27.0 1.3 %collective-permute-start.9 = (f32[192,128]{1,0:T(8,128)S(1)}, f32[192,128]{1,0:T(8,128)S(1)}, u32[]{:S(2)}, u32[]{:S(2)}) collective-permute-start(f32[192,128]{1,0:T(8,128)S(1)} %gram.1.own_pack), channel_id=1, source_target_pairs={{0,1},{1,0},{2,3},{3,2},{4,5},{5,4},{6,7},{7,6},{8,9},{9,8},{10,11... | collective-permute-start | bytes 294920 | tf_op jit(solution)/shard_map/ppermute | solution.py:268
  27.8 1.4 %collective-permute-start.8 = (f32[128,128]{1,0:T(8,128)S(1)}, f32[128,128]{1,0:T(8,128)S(1)}, u32[]{:S(2)}, u32[]{:S(2)}) collective-permute-start(f32[128,128]{1,0:T(8,128)S(1)} %get-tuple-element.41.part_ref), channel_id=1, source_target_pairs={{0,1},{1,0},{2,3},{3,2},{4,5},{5,4},{6,7},{7,6},{8,9},{9,8},{10,11... | collective-permute-start | bytes 196616 | tf_op jit(solution)/shard_map/ppermute | solution.py:268
  30.3 5.4 %collective-permute-start.12 = (f32[128,128]{1,0:T(8,128)S(1)}, f32[128,128]{1,0:T(8,128)S(1)}, u32[]{:S(2)}, u32[]{:S(2)}) collective-permute-start(f32[128,128]{1,0:T(8,128)S(1)} %get-tuple-element.44), channel_id=1, source_target_pairs={{0,24},{1,25},{2,26},{3,27},{4,28},{5,29},{6,30},{7,31},{8,16},{9,... | collective-permute-start | bytes 196616 | tf_op jit(solution)/shard_map/ppermute | solution.py:268
  32.1 4.9 %collective-permute-start.11 = (f32[128,128]{1,0:T(8,128)S(1)}, f32[128,128]{1,0:T(8,128)S(1)}, u32[]{:S(2)}, u32[]{:S(2)}) collective-permute-start(f32[128,128]{1,0:T(8,128)S(1)} %get-tuple-element.44), channel_id=1, source_target_pairs={{0,17},{1,16},{2,19},{3,18},{4,21},{5,20},{6,23},{7,22},{8,25},{9,... | collective-permute-start | bytes 196616 | tf_op jit(solution)/shard_map/ppermute | solution.py:268
  33.0 4.0 %collective-permute-start.10 = (f32[128,128]{1,0:T(8,128)S(1)}, f32[128,128]{1,0:T(8,128)S(1)}, u32[]{:S(2)}, u32[]{:S(2)}) collective-permute-start(f32[128,128]{1,0:T(8,128)S(1)} %get-tuple-element.44), channel_id=1, source_target_pairs={{0,9},{1,8},{2,11},{3,10},{4,13},{5,12},{6,15},{7,14},{8,1},{9,0},... | collective-permute-start | bytes 196616 | tf_op jit(solution)/shard_map/ppermute | solution.py:268
  37.0 6.8 %collective-permute-start.15 = (f32[128,128]{1,0:T(8,128)S(1)}, f32[128,128]{1,0:T(8,128)S(1)}, u32[]{:S(2)}, u32[]{:S(2)}) collective-permute-start(f32[128,128]{1,0:T(8,128)S(1)} %add_add_fusion.5), channel_id=1, source_target_pairs={{0,6},{1,7},{2,4},{3,5},{4,2},{5,3},{6,0},{7,1},{8,14},{9,15},{10,... | collective-permute-start | bytes 196616 | tf_op jit(solution)/shard_map/ppermute | solution.py:268
  40.7 5.3 %collective-permute-start.14 = (f32[128,128]{1,0:T(8,128)S(1)}, f32[128,128]{1,0:T(8,128)S(1)}, u32[]{:S(2)}, u32[]{:S(2)}) collective-permute-start(f32[128,128]{1,0:T(8,128)S(1)} %add_add_fusion.5), channel_id=1, source_target_pairs={{0,2},{1,3},{2,0},{3,1},{4,6},{5,7},{6,4},{7,5},{8,10},{9,11},{10,... | collective-permute-start | bytes 196616 | tf_op jit(solution)/shard_map/ppermute | solution.py:268
  40.7 5.9 %collective-permute-start.13 = (f32[128,128]{1,0:T(8,128)S(1)}, f32[128,128]{1,0:T(8,128)S(1)}, u32[]{:S(2)}, u32[]{:S(2)}) collective-permute-start(f32[128,128]{1,0:T(8,128)S(1)} %add_add_fusion.5), channel_id=1, source_target_pairs={{0,4},{1,5},{2,6},{3,7},{4,0},{5,1},{6,2},{7,3},{8,12},{9,13},{10,... | collective-permute-start | bytes 196616 | tf_op jit(solution)/shard_map/ppermute | solution.py:268
  47.3 1.3 %collective-permute-start.16 = (f32[128,128]{1,0:T(8,128)S(1)}, f32[128,128]{1,0:T(8,128)S(1)}, u32[]{:S(2)}, u32[]{:S(2)}) collective-permute-start(f32[128,128]{1,0:T(8,128)S(1)} %get-tuple-element.48.part_ref), channel_id=1, source_target_pairs={{0,1},{1,0},{2,3},{3,2},{4,5},{5,4},{6,7},{7,6},{8,9},{9,8},{10,11... | collective-permute-start | bytes 196616 | tf_op jit(solution)/shard_map/ppermute | solution.py:268
  49.7 5.3 %collective-permute-start.19 = (f32[128,128]{1,0:T(8,128)S(1)}, f32[128,128]{1,0:T(8,128)S(1)}, u32[]{:S(2)}, u32[]{:S(2)}) collective-permute-start(f32[128,128]{1,0:T(8,128)S(1)} %get-tuple-element.50), channel_id=1, source_target_pairs={{0,24},{1,25},{2,26},{3,27},{4,28},{5,29},{6,30},{7,31},{8,16},{9,... | collective-permute-start | bytes 196616 | tf_op jit(solution)/shard_map/ppermute | solution.py:268
  51.6 4.7 %collective-permute-start.18 = (f32[128,128]{1,0:T(8,128)S(1)}, f32[128,128]{1,0:T(8,128)S(1)}, u32[]{:S(2)}, u32[]{:S(2)}) collective-permute-start(f32[128,128]{1,0:T(8,128)S(1)} %get-tuple-element.50), channel_id=1, source_target_pairs={{0,17},{1,16},{2,19},{3,18},{4,21},{5,20},{6,23},{7,22},{8,25},{9,... | collective-permute-start | bytes 196616 | tf_op jit(solution)/shard_map/ppermute | solution.py:268
  52.2 4.1 %collective-permute-start.17 = (f32[128,128]{1,0:T(8,128)S(1)}, f32[128,128]{1,0:T(8,128)S(1)}, u32[]{:S(2)}, u32[]{:S(2)}) collective-permute-start(f32[128,128]{1,0:T(8,128)S(1)} %get-tuple-element.50), channel_id=1, source_target_pairs={{0,9},{1,8},{2,11},{3,10},{4,13},{5,12},{6,15},{7,14},{8,1},{9,0},... | collective-permute-start | bytes 196616 | tf_op jit(solution)/shard_map/ppermute | solution.py:268
  56.3 6.8 %collective-permute-start.22 = (f32[128,128]{1,0:T(8,128)S(1)}, f32[128,128]{1,0:T(8,128)S(1)}, u32[]{:S(2)}, u32[]{:S(2)}) collective-permute-start(f32[128,128]{1,0:T(8,128)S(1)} %add_add_fusion.3), channel_id=1, source_target_pairs={{0,6},{1,7},{2,4},{3,5},{4,2},{5,3},{6,0},{7,1},{8,14},{9,15},{10,... | collective-permute-start | bytes 196616 | tf_op jit(solution)/shard_map/ppermute | solution.py:268
  58.7 6.3 %collective-permute-start.21 = (f32[128,128]{1,0:T(8,128)S(1)}, f32[128,128]{1,0:T(8,128)S(1)}, u32[]{:S(2)}, u32[]{:S(2)}) collective-permute-start(f32[128,128]{1,0:T(8,128)S(1)} %add_add_fusion.3), channel_id=1, source_target_pairs={{0,2},{1,3},{2,0},{3,1},{4,6},{5,7},{6,4},{7,5},{8,10},{9,11},{10,... | collective-permute-start | bytes 196616 | tf_op jit(solution)/shard_map/ppermute | solution.py:268
  59.0 6.6 %collective-permute-start.20 = (f32[128,128]{1,0:T(8,128)S(1)}, f32[128,128]{1,0:T(8,128)S(1)}, u32[]{:S(2)}, u32[]{:S(2)}) collective-permute-start(f32[128,128]{1,0:T(8,128)S(1)} %add_add_fusion.3), channel_id=1, source_target_pairs={{0,4},{1,5},{2,6},{3,7},{4,0},{5,1},{6,2},{7,3},{8,12},{9,13},{10,... | collective-permute-start | bytes 196616 | tf_op jit(solution)/shard_map/ppermute | solution.py:268
  66.3 1.3 %collective-permute-start.23 = (f32[128,128]{1,0:T(8,128)S(1)}, f32[128,128]{1,0:T(8,128)S(1)}, u32[]{:S(2)}, u32[]{:S(2)}) collective-permute-start(f32[128,128]{1,0:T(8,128)S(1)} %get-tuple-element.54.part_ref), channel_id=1, source_target_pairs={{0,1},{1,0},{2,3},{3,2},{4,5},{5,4},{6,7},{7,6},{8,9},{9,8},{10,11... | collective-permute-start | bytes 196616 | tf_op jit(solution)/shard_map/ppermute | solution.py:268
  68.6 5.3 %collective-permute-start.26 = (f32[128,128]{1,0:T(8,128)S(1)}, f32[128,128]{1,0:T(8,128)S(1)}, u32[]{:S(2)}, u32[]{:S(2)}) collective-permute-start(f32[128,128]{1,0:T(8,128)S(1)} %get-tuple-element.56), channel_id=1, source_target_pairs={{0,24},{1,25},{2,26},{3,27},{4,28},{5,29},{6,30},{7,31},{8,16},{9,... | collective-permute-start | bytes 196616 | tf_op jit(solution)/shard_map/ppermute | solution.py:268
  70.4 4.8 %collective-permute-start.25 = (f32[128,128]{1,0:T(8,128)S(1)}, f32[128,128]{1,0:T(8,128)S(1)}, u32[]{:S(2)}, u32[]{:S(2)}) collective-permute-start(f32[128,128]{1,0:T(8,128)S(1)} %get-tuple-element.56), channel_id=1, source_target_pairs={{0,17},{1,16},{2,19},{3,18},{4,21},{5,20},{6,23},{7,22},{8,25},{9,... | collective-permute-start | bytes 196616 | tf_op jit(solution)/shard_map/ppermute | solution.py:268
  71.1 4.1 %collective-permute-start.24 = (f32[128,128]{1,0:T(8,128)S(1)}, f32[128,128]{1,0:T(8,128)S(1)}, u32[]{:S(2)}, u32[]{:S(2)}) collective-permute-start(f32[128,128]{1,0:T(8,128)S(1)} %get-tuple-element.56), channel_id=1, source_target_pairs={{0,9},{1,8},{2,11},{3,10},{4,13},{5,12},{6,15},{7,14},{8,1},{9,0},... | collective-permute-start | bytes 196616 | tf_op jit(solution)/shard_map/ppermute | solution.py:268
  75.2 6.9 %collective-permute-start.29 = (f32[128,128]{1,0:T(8,128)S(1)}, f32[128,128]{1,0:T(8,128)S(1)}, u32[]{:S(2)}, u32[]{:S(2)}) collective-permute-start(f32[128,128]{1,0:T(8,128)S(1)} %add_add_fusion.1), channel_id=1, source_target_pairs={{0,6},{1,7},{2,4},{3,5},{4,2},{5,3},{6,0},{7,1},{8,14},{9,15},{10,... | collective-permute-start | bytes 196616 | tf_op jit(solution)/shard_map/ppermute | solution.py:268
  77.5 6.5 %collective-permute-start.28 = (f32[128,128]{1,0:T(8,128)S(1)}, f32[128,128]{1,0:T(8,128)S(1)}, u32[]{:S(2)}, u32[]{:S(2)}) collective-permute-start(f32[128,128]{1,0:T(8,128)S(1)} %add_add_fusion.1), channel_id=1, source_target_pairs={{0,2},{1,3},{2,0},{3,1},{4,6},{5,7},{6,4},{7,5},{8,10},{9,11},{10,... | collective-permute-start | bytes 196616 | tf_op jit(solution)/shard_map/ppermute | solution.py:268
  77.6 6.7 %collective-permute-start.27 = (f32[128,128]{1,0:T(8,128)S(1)}, f32[128,128]{1,0:T(8,128)S(1)}, u32[]{:S(2)}, u32[]{:S(2)}) collective-permute-start(f32[128,128]{1,0:T(8,128)S(1)} %add_add_fusion.1), channel_id=1, source_target_pairs={{0,4},{1,5},{2,6},{3,7},{4,0},{5,1},{6,2},{7,3},{8,12},{9,13},{10,... | collective-permute-start | bytes 196616 | tf_op jit(solution)/shard_map/ppermute | solution.py:268
  79.7 4.6 %collective-permute-start.31 = (f32[384,128]{1,0:T(8,128)S(1)}, f32[384,128]{1,0:T(8,128)S(1)}, u32[]{:S(2)}, u32[]{:S(2)}) collective-permute-start(f32[384,128]{1,0:T(8,128)S(1)} %affine.1.own_ref.own_base), channel_id=1, source_target_pairs={{0,1},{1,0},{2,3},{3,2},{4,5},{5,4},{6,7},{7,6},{8,9},{9,8},{10,11... | collective-permute-start | bytes 589832 | tf_op jit(solution)/shard_map/ppermute | solution.py:268
  84.3 2.6 %collective-permute-start.30 = (f32[128,128]{1,0:T(8,128)S(1)}, f32[128,128]{1,0:T(8,128)S(1)}, u32[]{:S(2)}, u32[]{:S(2)}) collective-permute-start(f32[128,128]{1,0:T(8,128)S(1)} %add_add_fusion.own_ref), channel_id=1, source_target_pairs={{0,1},{1,0},{2,3},{3,2},{4,5},{5,4},{6,7},{7,6},{8,9},{9,8},{10,11... | collective-permute-start | bytes 196616 | tf_op jit(solution)/shard_map/ppermute | solution.py:268
